TPU v7x, 128 devices: a whole 4x4x4 slice. The times are simulated.
128 devices in a mesh: tm: 16 (over z_lo, y, core), chan: 8 (over x, z_hi).
Axes of the slice: x: 4, y: 4, z: 4 (z_hi: 2, z_lo: 2; z = z_hi * 2 + z_lo), core: 2. Of those that a mesh axis runs over, the one named last changes fastest.
Arguments:
- auxiliary: float32 [512, 524288], P('chan', 'tm'), may hold values from -30 to 30
- proofs: float32 [64, 524288], P('chan', 'tm'), may hold values from -12 to 12
Outputs:
- coherence: float32 [512, 64, 4096], P('chan', None, 'tm')
All inputs are finite; a program needn't handle non-finite values.
Results may differ from a plain program's by a relative error of at most 0.00076.
Values may be sent and summed in bfloat16 or wider, within the bound.
A program may use at most 192 MiB of HBM per device.

v0:
```python
import math

import jax
import jax.numpy as jnp
from jax import lax
from jax.sharding import PartitionSpec as P

SEG_LEN = 8192
FACTOR = 64
STRIDE = 4096
BINS = 4096


def shifted(value, axis, by):
    peers = lax.axis_size(axis)
    pairs = [(i, i + by) for i in range(peers) if 0 <= i + by < peers]
    return lax.ppermute(value, axis, pairs)


def angle_table(left_count, right_count, modulus):
    left_index = jnp.arange(left_count, dtype=jnp.int32)
    right_index = jnp.arange(right_count, dtype=jnp.int32)
    product = left_index[:, None] * right_index[None, :] % modulus
    return 2.0 * math.pi / modulus * product.astype(jnp.float32)


def transform_block(windowed):
    row_count = windowed.shape[0]
    second = SEG_LEN // FACTOR
    highest = lax.Precision.HIGHEST
    angle_first = angle_table(FACTOR, FACTOR, FACTOR)
    angle_twist = angle_table(FACTOR, second, SEG_LEN)
    angle_second = angle_table(second, second // 2, second)
    cos_twist = jnp.cos(angle_twist)
    sin_twist = jnp.sin(angle_twist)
    cos_second = jnp.cos(angle_second)
    sin_second = jnp.sin(angle_second)
    shaped = windowed.reshape(row_count, FACTOR, second)
    real_one = jnp.einsum("rpq,pk->rkq", shaped, jnp.cos(angle_first), precision=highest)
    imag_one = -jnp.einsum("rpq,pk->rkq", shaped, jnp.sin(angle_first), precision=highest)
    real_two = real_one * cos_twist + imag_one * sin_twist
    imag_two = imag_one * cos_twist - real_one * sin_twist
    real_out = jnp.einsum("rkq,qm->rmk", real_two, cos_second, precision=highest) + jnp.einsum(
        "rkq,qm->rmk", imag_two, sin_second, precision=highest
    )
    imag_out = jnp.einsum("rkq,qm->rmk", imag_two, cos_second, precision=highest) - jnp.einsum(
        "rkq,qm->rmk", real_two, sin_second, precision=highest
    )
    return (real_out.reshape(row_count, BINS), imag_out.reshape(row_count, BINS))


def transform(windowed):
    row_count = windowed.shape[0]
    block_rows = math.gcd(row_count, 64)
    blocks = windowed.reshape(row_count // block_rows, block_rows, SEG_LEN)
    real_out, imag_out = lax.map(transform_block, blocks)
    return (real_out.reshape(row_count, BINS), imag_out.reshape(row_count, BINS))


def segments_of(signal, seg_count):
    channels = signal.shape[0]
    blocks = signal.reshape(channels, seg_count + 1, STRIDE)
    segments = jnp.concatenate([blocks[:, :-1], blocks[:, 1:]], axis=2)
    position = jnp.arange(SEG_LEN, dtype=jnp.float32)
    window = 0.5 - 0.5 * jnp.cos(2.0 * math.pi * position / SEG_LEN)
    return (segments * window).reshape(channels * seg_count, SEG_LEN)


def channel_totals(local_sums):
    return lax.psum((local_sums[0], local_sums[1]), "tm")


def coherence_block(aux_moved, aux_power, wit_piece):
    left_real = jnp.concatenate([aux_moved[0], aux_moved[1]], axis=1)
    left_imag = jnp.concatenate([aux_moved[1], -aux_moved[0]], axis=1)
    right_side = jnp.concatenate([wit_piece[0], wit_piece[1]], axis=1)
    cross_real = jnp.einsum(
        "csf,wsf->cwf", left_real, right_side, preferred_element_type=jnp.float32
    )
    cross_imag = jnp.einsum(
        "csf,wsf->cwf", left_imag, right_side, preferred_element_type=jnp.float32
    )
    wit_float = wit_piece.astype(jnp.float32)
    wit_power = jnp.sum(wit_float * wit_float, axis=(0, 2))
    return (cross_real * cross_real + cross_imag * cross_imag) / (
        (aux_power[:, None, :] + 1e-06) * (wit_power[None, :, :] + 1e-06)
    )


def per_device(auxiliary, proofs):
    aux_rows = auxiliary.shape[0]
    seg_count = auxiliary.shape[1] // STRIDE
    tm_size = lax.axis_size("tm")
    next_aux, next_wit = shifted((auxiliary[:, :STRIDE], proofs[:, :STRIDE]), "tm", -1)
    signal = jnp.concatenate(
        [
            jnp.concatenate([auxiliary, next_aux], axis=1),
            jnp.concatenate([proofs, next_wit], axis=1),
        ],
        axis=0,
    )
    channels = signal.shape[0]
    local_sums = (jnp.sum(auxiliary, axis=1), jnp.sum(proofs, axis=1))
    total_samples = auxiliary.shape[1] * tm_size
    totals = channel_totals(local_sums)
    channel_means = jnp.concatenate(totals) / total_samples
    real_part, imag_part = transform(segments_of(signal - channel_means[:, None], seg_count))
    spectra = (
        jnp.stack([real_part, imag_part]).astype(jnp.bfloat16).reshape(2, channels, seg_count, BINS)
    )
    aux_spec = spectra[:, :aux_rows]
    wit_spec = spectra[:, aux_rows:]
    aux_moved, wit_moved = (
        lax.all_to_all(aux_spec, "tm", split_axis=3, concat_axis=2, tiled=True),
        lax.all_to_all(wit_spec, "tm", split_axis=3, concat_axis=2, tiled=True),
    )
    kept_segments = seg_count * tm_size - 1
    aux_moved = aux_moved[:, :, :kept_segments]
    wit_moved = wit_moved[:, :, :kept_segments]
    aux_float = aux_moved.astype(jnp.float32)
    aux_power = jnp.sum(aux_float * aux_float, axis=(0, 2))
    return coherence_block(
        aux_moved, aux_power, lax.all_gather(wit_moved, "chan", axis=1, tiled=True)
    )


def solution(mesh):
    return jax.shard_map(
        per_device,
        mesh=mesh,
        in_specs=(P("chan", "tm"), P("chan", "tm")),
        out_specs=P("chan", None, "tm"),
        check_vma=False,
    )
```

profile of v0, /device:TPU:1, one launch (start us, length us, event | category | flops | bytes accessed | tf_op | source)
XLA Modules:
  0.0 844.6 jit_solution(2119324733593053343)
XLA Ops:
  18.4 28.1 %all-reduce = (f32[8]{0:T(128)S(1)}, f32[64]{0:T(128)S(1)}) all-reduce(f32[8]{0:T(128)S(1)} %reduce_sum.37, f32[64]{0:T(128)S(1)} %reduce_sum.36), channel_id=1, replica_groups=mesh['tm'=16,'chan'=8] {'tm'}, use_global_device_ids=true, to_apply=%region_3.0 | all-reduce | flops 72 | bytes 576 | tf_op jit(solution)/shard_map/psum | solution.py:70
  47.6 7.6 pad_maximum_fusion
  55.2 11.2 %concatenate.41 = f32[64,9,4096]{2,1,0:T(8,128)} reshape(f32[64,36864]{1,0:T(8,128)} %pad_maximum_fusion) | data formatting | bytes 18874368 | tf_op jit(solution)/shard_map/concatenate | solution.py:95
  66.4 6.7 maximum_subtract_fusion
  73.1 6.9 fusion.86
  80.0 12.8 %maximum_multiply_fusion = f32[9,64,8192]{2,1,0:T(8,128)} fusion(f32[9,64,4096]{2,1,0:T(8,128)} %bitcast.110, f32[9,64,4096]{2,1,0:T(8,128)} %bitcast.109, f32[8192]{0:T(1024)S(1)} %multiply_subtract_fusion.3), kind=kLoop, calls=%fused_computation.81 | loop fusion | flops 9437184 | bytes 37781504 | tf_op jit(solution)/shard_map/mul | solution.py:66
  92.9 354.9 %while.15 = (s32[]{:T(128)}, bf16[9,64,4096]{2,1,0:T(8,128)(2,1)}, bf16[9,64,4096]{2,1,0:T(8,128)(2,1)}, f32[9,64,8192]{2,1,0:T(8,128)}, s32[]{:T(128)}) while((s32[]{:T(128)}, bf16[9,64,4096]{2,1,0:T(8,128)(2,1)}, bf16[9,64,4096]{2,1,0:T(8,128)(2,1)}, f32[9,64,8192]{2,1,0:T(8,128)}, s32[]{:T(128)}) %tuple.35), condition=%wide.region_5.6_spmd, body=%wide.region_4.5_spmd.sunk | while | flops 2426159104 | bytes 60097144 | solution.py:56
  128.1 7.9 fusion.124
  165.9 7.9 fusion.124
  203.7 7.9 fusion.124
  241.4 7.9 fusion.124
  279.2 7.9 fusion.124
  317.0 7.9 fusion.124
  354.8 7.9 fusion.124
  392.6 7.9 fusion.124
  430.3 7.9 fusion.124
  449.1 13.8 %copy.45 = bf16[2,8,8,4096]{2,1,0,3:T(8,128)(2,1)} copy(bf16[2,8,8,4096]{3,2,1,0:T(8,128)(2,1)S(1)} %pad_maximum_fusion.6) | data formatting | bytes 2097152 | tf_op jit(solution)/shard_map/slice | solution.py:112
  462.9 19.8 %reshape.96 = bf16[16,2,16384]{2,1,0:T(2,128)(2,1)S(1)} reshape(bf16[4096,2,8,8]{3,2,1,0:T(8,128)(2,1)} %bitcast.107) | data formatting | bytes 2097152
  482.7 24.6 %all_to_all.36 = bf16[16,2,16384]{2,1,0:T(2,128)(2,1)S(1)} all-to-all(bf16[16,2,16384]{2,1,0:T(2,128)(2,1)S(1)} %reshape.96), channel_id=1, replica_groups=mesh['tm'=16,'chan'=8] {'tm'}, dimensions={0} | all-to-all | bytes 2097152 | tf_op jit(solution)/shard_map/all_to_all | solution.py:115
  507.3 20.9 %reshape.97 = bf16[4096,2,8,8]{3,2,1,0:T(8,128)(2,1)} reshape(bf16[16,2,16384]{2,1,0:T(2,128)(2,1)S(1)} %all_to_all.36) | data formatting | bytes 2097152
  528.2 16.0 %copy.47 = bf16[2,8,16,8,256]{4,3,2,1,0:T(8,128)(2,1)S(1)} copy(bf16[2,8,16,8,256]{3,1,0,4,2:T(8,128)(2,1)} %bitcast.108) | data formatting | bytes 2097152 | tf_op jit(solution)/shard_map/all_to_all | solution.py:115
  545.7 7.6 pad_maximum_fusion.1
  553.3 24.6 %copy.49 = bf16[2,64,8,4096]{1,2,0,3:T(8,128)(2,1)} copy(bf16[2,64,8,4096]{3,2,1,0:T(8,128)(2,1)} %pad_maximum_fusion.1) | data formatting | bytes 16777216 | tf_op jit(solution)/shard_map/slice | solution.py:111
  577.9 19.7 %reshape.94 = bf16[16,2,131072]{2,1,0:T(2,128)(2,1)} reshape(bf16[4096,2,8,64]{3,2,1,0:T(8,128)(2,1)} %bitcast.105) | data formatting | bytes 16777216
  597.6 121.7 %all_to_all.37 = bf16[16,2,131072]{2,1,0:T(2,128)(2,1)} all-to-all(bf16[16,2,131072]{2,1,0:T(2,128)(2,1)} %reshape.94), channel_id=1, replica_groups=mesh['tm'=16,'chan'=8] {'tm'}, dimensions={0} | all-to-all | bytes 16777216 | tf_op jit(solution)/shard_map/all_to_all | solution.py:114
  719.3 19.3 %reshape.95 = bf16[4096,2,8,64]{3,2,1,0:T(8,128)(2,1)} reshape(bf16[16,2,131072]{2,1,0:T(2,128)(2,1)} %all_to_all.37) | data formatting | bytes 16777216
  738.6 22.7 %copy.51 = bf16[2,64,16,8,256]{4,3,2,1,0:T(8,128)(2,1)} copy(bf16[2,64,16,8,256]{1,3,0,4,2:T(8,128)(2,1)} %bitcast.106) | data formatting | bytes 16777216 | tf_op jit(solution)/shard_map/all_to_all | solution.py:114
  767.3 6.7 copy.63
  796.9 7.5 slice_bitcast_fusion.1
  805.8 10.5 %fusion.74 = f32[256,64,64]{2,1,0:T(8,128)} fusion(bf16[64,127,256]{1,0,2:T(8,128)(2,1)S(1)} %bitcast.118, bf16[64,127,256]{1,0,2:T(8,128)(2,1)S(1)} %bitcast.115, bf16[64,127,256]{1,0,2:T(8,128)(2,1)} %get-tuple-element.100, bf16[64,127,256]{1,0,2:T(8,128)(2,1)} %get-tuple-element.99), kind=kOutput, calls=%fused_computation.87 | convolution fusion | flops 565968896 | bytes 20840448 | tf_op jit(solution)/shard_map/csf,wsf->cwf/dot_general | solution.py:77
  816.3 12.6 %bitcast_divide_fusion = f32[64,64,256]{0,1,2:T(8,128)} fusion(f32[256,64,64]{2,1,0:T(8,128)} %fusion.74, f32[64,256]{0,1:T(8,128)S(1)} %copy.56, f32[64,256]{0,1:T(8,128)S(1)} %copy.54, bf16[64,127,256]{1,0,2:T(8,128)(2,1)S(1)} %copy-done.5, bf16[64,127,256]{1,0,2:T(8,128)(2,1)S(1)} %bitcast.119, bf16[64,127,256]{1,0,2:T(8,128)(2,1)} %get-tuple-element.100, ...), kind=kOutput, calls=%fused_computation.95 | convolution fusion | flops 571211776 | bytes 25165824 | tf_op jit(solution)/shard_map/csf,wsf->cwf/dot_general | solution.py:80
  828.9 8.6 %copy.57 = f32[64,64,256]{2,1,0:T(8,128)} copy(f32[64,64,256]{0,1,2:T(8,128)} %bitcast_divide_fusion) | data formatting | bytes 8388608 | tf_op jit(solution)/shard_map/div | solution.py:85
  (181 shorter events, 314.3 us)
Async XLA Ops:
  6.5 784.3 %all-gather.2.cloned.1.call-start = ((), (), s32[]{:S(2)}) async-start(), calls=%async_computation.2 | async-start | bytes 9437184 | tf_op jit(solution)/shard_map/all_gather | solution.py:123
  8.8 7.3 copy-start.3
  8.8 38.8 %collective-permute-start = (f32[64,4096]{1,0:T(8,128)}, f32[64,4096]{1,0:T(8,128)S(1)}, u32[]{:S(2)}, u32[]{:S(2)}) collective-permute-start(f32[64,4096]{1,0:T(8,128)} %slice.40), channel_id=1, source_target_pairs={{8,0},{16,8},{24,16},{32,24},{40,32},{48,40},{56,48},{64,56},{72,6... | collective-permute-start | bytes 3145736 | tf_op jit(solution)/shard_map/ppermute | solution.py:17
  16.5 30.2 %collective-permute-start.1 = (f32[8,4096]{1,0:T(8,128)S(1)}, f32[8,4096]{1,0:T(8,128)S(1)}, u32[]{:S(2)}, u32[]{:S(2)}) collective-permute-start(f32[8,4096]{1,0:T(8,128)S(1)} %slice.41), channel_id=1, source_target_pairs={{8,0},{16,8},{24,16},{32,24},{40,32},{48,40},{56,48},{64,56},{72,6... | collective-permute-start | bytes 393224 | tf_op jit(solution)/shard_map/ppermute | solution.py:17
  113.7 6.5 copy-start
  128.1 7.9 copy-start.1
  151.5 6.5 copy-start
  165.9 7.9 copy-start.1
  189.3 6.5 copy-start
  203.7 7.9 copy-start.1
  227.1 6.5 copy-start
  241.4 7.9 copy-start.1
  264.9 6.5 copy-start
  279.2 7.9 copy-start.1
  302.6 6.5 copy-start
  317.0 7.9 copy-start.1
  340.4 6.5 copy-start
  354.8 7.9 copy-start.1
  378.2 6.5 copy-start
  392.6 7.9 copy-start.1
  416.0 6.5 copy-start
  430.3 7.9 copy-start.1
  796.9 7.5 copy-start.2
  796.9 8.8 %copy-start.4 = (bf16[1,64,127,256]{2,1,3,0:T(8,128)(2,1)S(1)}, bf16[1,64,127,256]{2,1,3,0:T(8,128)(2,1)}, u32[]{:S(2)}) copy-start(bf16[1,64,127,256]{2,1,3,0:T(8,128)(2,1)} %copy.64) | copy-start | bytes 12484612
  805.8 10.5 %copy-start.5 = (bf16[64,127,256]{1,0,2:T(8,128)(2,1)S(1)}, bf16[64,127,256]{1,0,2:T(8,128)(2,1)}, u32[]{:S(2)}) copy-start(bf16[64,127,256]{1,0,2:T(8,128)(2,1)} %bitcast_negate_fusion) | copy-start | bytes 12484612
Sparse Core Ops, SparseCore 0:
  545.9 208.4 all-gather.1
where the time goes:
time: 853 us; the launch traced here: 845 us
  matrix products  300 us (35%)
  local copies, waits for them, and re-layouts  276 us (32%)
  blocking collectives  174 us (20%)
  other arithmetic  59.1 us (7%)
  loops' own time  15.5 us (2%)
  between operations  13.8 us (2%)
    all_to_all x1, blocking collectives, per_device(): lax.all_to_all(aux_spec, 'tm', split_axis=3, concat_axis=2, tiled=True)  122 us
    unnamed x15, local copies, waits for them, and re-layouts  95.7 us
    dot_general x9, matrix products, transform_block(): jnp.einsum('rkq,qm->rmk', imag_two, cos_second, precision=highest)  71.1 us
    dot_general x9, matrix products, transform_block(): jnp.einsum('rkq,qm->rmk', real_two, sin_second, precision=highest)  56.3 us
    dot_general x9, matrix products, transform_block(): jnp.einsum('rkq,qm->rmk', real_two, cos_second, precision=highest)  56 us
    dot_general x9, matrix products, transform_block(): jnp.einsum('rkq,qm->rmk', imag_two, sin_second, precision=highest)  55.9 us
    psum x1, blocking collectives, channel_totals(): return lax.psum((local_sums[0], local_sums[1]), 'tm')  28.1 us
    all_to_all x1, blocking collectives, per_device(): lax.all_to_all(wit_spec, 'tm', split_axis=3, concat_axis=2, tiled=True)  24.6 us
  transfers between devices with their start and end apart: 3, of which 0 were waited for; matrix products, arithmetic and copies ran while one was open for 15% of the time, Pallas kernels for 0%

commit v1 on v0

v1 whole, which is shorter than its diff:
```python
import math
import functools
import numpy as np
import jax
import jax.numpy as jnp
from jax import lax
from jax.sharding import PartitionSpec as P
from jax.experimental import pallas as pl
from jax.experimental.pallas import tpu as pltpu

NT = (((1,), (1,)), ((), ()))
PITCH = 72


def split(x):
    hi = x.astype(jnp.bfloat16)
    lo = (x - hi.astype(jnp.float32)).astype(jnp.bfloat16)
    return hi, lo


def np_split(x):
    x = jnp.asarray(x, jnp.float32)
    return split(x)


def fft_tables():
    a = np.arange(64)
    ang = 2 * np.pi * np.outer(a, a) % (2 * np.pi * 64) / 64
    ang = 2 * np.pi * (np.outer(a, a) % 64) / 64
    f1 = np.concatenate([np.cos(ang), -np.sin(ang)], 0)
    h, l = np_split(f1)
    f1cat = jnp.concatenate([h, h, l, l], axis=1)
    lane = np.arange(128)
    k2 = np.arange(32)
    ang2 = 2 * np.pi * (np.outer(k2, lane) % 64) / 64
    re = np.concatenate([np.cos(ang2), np.sin(ang2)], 1)
    im = np.concatenate([-np.sin(ang2), np.cos(ang2)], 1)
    h, l = np_split(np.concatenate([re, im], 0))
    w2 = jnp.concatenate([h, l], axis=0)
    k1 = np.arange(128)
    angt = 2 * np.pi * (np.outer(k1, lane) % 8192) / 8192
    cos_t = jnp.asarray(np.cos(angt), jnp.float32)
    sin_t = jnp.asarray(np.sin(angt), jnp.float32)
    n = np.arange(8192)
    hann = jnp.asarray((0.5 - 0.5 * np.cos(2 * np.pi * n / 8192)).reshape(64, 128), jnp.float32)
    return f1cat, w2, cos_t, sin_t, hann


def fft_step(x2d, base, mean8, scr, s, tabs):
    f1, w2, cos_t, sin_t, hann = tabs
    cats = []
    for c in range(8):
        xs = (x2d[pl.ds(base + s * 256 + c, 64, stride=8), :] - mean8[c:c + 1]) * hann[...]
        h, l = split(xs)
        cats.append(jnp.concatenate([h, l, h, l], axis=0))
    y = jnp.dot(f1[...], jnp.concatenate(cats, axis=1), preferred_element_type=jnp.float32)
    zh, zl = [], []
    for c in range(8):
        yre = y[:64, 128 * c:128 * c + 128]
        yim = y[64:, 128 * c:128 * c + 128]
        for b in range(2):
            ct = cos_t[64 * b:64 * b + 64]
            st = sin_t[64 * b:64 * b + 64]
            h, l = split(jnp.concatenate([yre * ct + yim * st, yim * ct - yre * st], axis=1))
            zh.append(h)
            zl.append(l)
    w = w2[...]
    a = lax.dot_general(w, jnp.concatenate(zh, axis=0), NT, preferred_element_type=jnp.float32)
    b = lax.dot_general(w[:64], jnp.concatenate(zl, axis=0), NT, preferred_element_type=jnp.float32)
    o = a[:64] + a[64:] + b
    for c in range(8):
        scr[pl.ds(c * 8 + s, 64, stride=PITCH), :] = o[:, 128 * c:128 * c + 128]


def spectra_kernel(peers, aux, wit, f1, w2, cos_t, sin_t, hann, recv, x, scr, send, sums, means,
                   load_sem, halo_send, halo_recv, sum_send, sum_recv, send_sem, recv_sem, own_sem):
    tabs = (f1, w2, cos_t, sin_t, hann)
    me = lax.axis_index("tm")
    before = lax.rem(me + peers - 1, peers)
    blocks = x.shape[0]

    def source(b):
        return wit.at[0] if b == 0 else aux.at[b - 1]

    loads = []
    for b in range(blocks):
        cp = pltpu.make_async_copy(source(b), x.at[b, pl.ds(0, 256)], load_sem.at[b])
        cp.start()
        loads.append(cp)
    barrier = pltpu.get_barrier_semaphore()

    def greet(j, _):
        pl.semaphore_signal(barrier, inc=1, device_id={"tm": lax.rem(me + j, peers)},
                            device_id_type=pl.DeviceIdType.MESH)
        return 0

    lax.fori_loop(1, peers, greet, 0)
    pl.semaphore_wait(barrier, peers - 1)

    halos = []
    for b in range(blocks):
        cp = pltpu.make_async_remote_copy(
            src_ref=source(b).at[pl.ds(0, 32)], dst_ref=x.at[b, pl.ds(256, 32)],
            send_sem=halo_send.at[b], recv_sem=halo_recv.at[b],
            device_id={"tm": before}, device_id_type=pl.DeviceIdType.MESH)
        cp.start()
        halos.append(cp)

    lane = lax.broadcasted_iota(jnp.int32, (8, 128), 1)
    total = jnp.zeros((8, 128), jnp.float32)
    for b in range(blocks):
        loads[b].wait()

        def add(i, acc):
            return acc + jnp.sum(x[b, pl.ds(i * 16, 16)], axis=0)

        part = lax.fori_loop(0, 16, add, jnp.zeros((8, 128), jnp.float32))
        total = jnp.where(lane == b, jnp.sum(part, axis=1, keepdims=True), total)
    sums[0] = total

    def sum_copy(j):
        return pltpu.make_async_remote_copy(
            src_ref=sums.at[0], dst_ref=sums.at[j], send_sem=sum_send.at[j], recv_sem=sum_recv.at[j],
            device_id={"tm": lax.rem(me + j, peers)}, device_id_type=pl.DeviceIdType.MESH)

    def sum_start(j, _):
        sum_copy(j).start()
        return 0

    def sum_wait(j, acc):
        sum_copy(j).wait()
        return acc + sums[j]

    lax.fori_loop(1, peers, sum_start, 0)
    total = lax.fori_loop(1, peers, sum_wait, total)
    mean = total / (256 * 128 * peers)
    for b in range(blocks):
        means[b] = jnp.broadcast_to(mean[:, b:b + 1], (8, 128))
    for b in range(blocks):
        halos[b].wait()

    x2d = x.reshape(blocks * 288 * 8, 128)
    row = lax.broadcasted_iota(jnp.int32, (64, 128), 0)
    keep = jnp.where((lax.rem(row, 8) == 7) & (me == peers - 1), 0.0, 1.0)

    def block_copy(b, j):
        slot = lax.rem(b, 2)
        to = lax.rem(me + j, peers)
        return pltpu.make_async_remote_copy(
            src_ref=send.at[slot, to], dst_ref=recv.at[b, me],
            send_sem=send_sem.at[slot, j], recv_sem=recv_sem.at[b, j],
            device_id={"tm": to}, device_id_type=pl.DeviceIdType.MESH)

    def own_copy(b):
        slot = lax.rem(b, 2)
        return pltpu.make_async_copy(send.at[slot, me], recv.at[b, me], own_sem.at[slot])

    def drain(b):
        def one(j, _):
            block_copy(b, j).wait_send()
            return 0
        lax.fori_loop(1, peers, one, 0)
        own_copy(b).wait()

    def block(b, _):
        slot = lax.rem(b, 2)
        mean8 = means[b]

        def step(s, _):
            fft_step(x2d, b * 2304, mean8, scr, s, tabs)
            return 0

        lax.fori_loop(0, 8, step, 0)

        @pl.when(b >= 2)
        def _():
            drain(b - 2)

        def pack(d, _):
            for part in range(2):
                for half in range(2):
                    at = pl.multiple_of((part * 32 + d * 2 + half) * PITCH, 8)
                    v = scr[pl.ds(at, 64), :] * keep
                    send[slot, d, part, :, half * 128:half * 128 + 128] = v.astype(jnp.bfloat16)
            return 0

        lax.fori_loop(0, peers, pack, 0)

        def go(j, _):
            block_copy(b, j).start()
            return 0

        lax.fori_loop(1, peers, go, 0)
        own_copy(b).start()
        return 0

    lax.fori_loop(0, blocks, block, 0)
    drain(blocks - 2)
    drain(blocks - 1)

    def landed(b, _):
        def one(j, _):
            block_copy(b, j).wait_recv()
            return 0
        return lax.fori_loop(1, peers, one, 0)

    lax.fori_loop(0, blocks, landed, 0)


def spectra(aux, wit, peers):
    tabs = fft_tables()
    vm = pl.BlockSpec(memory_space=pltpu.VMEM)
    hbm = pl.BlockSpec(memory_space=pl.ANY)
    blocks = aux.shape[0] + 1
    dma = pltpu.SemaphoreType.DMA
    return pl.pallas_call(
        functools.partial(spectra_kernel, peers),
        out_shape=jax.ShapeDtypeStruct((blocks, peers, 2, 64, 256), jnp.bfloat16),
        in_specs=[hbm, hbm] + [vm] * 5,
        out_specs=hbm,
        scratch_shapes=[
            pltpu.VMEM((blocks, 288, 8, 128), jnp.float32),
            pltpu.VMEM((64 * PITCH, 128), jnp.float32),
            pltpu.VMEM((2, peers, 2, 64, 256), jnp.bfloat16),
            pltpu.VMEM((peers, 8, 128), jnp.float32),
            pltpu.VMEM((blocks, 8, 128), jnp.float32),
            dma((blocks,)), dma((blocks,)), dma((blocks,)),
            dma((peers,)), dma((peers,)),
            dma((2, peers)), dma((blocks, peers)), dma((2,)),
        ],
        compiler_params=pltpu.CompilerParams(
            collective_id=0, has_side_effects=True, vmem_limit_bytes=62 * 2 ** 20),
    )(aux, wit, *tabs)


def gather_rows(stage, rows):
    def one(i, _):
        t = i // 2
        part = lax.rem(i, 2)
        v = stage[t, part].astype(jnp.float32)
        at = pl.multiple_of(part * 128 + t * 8, 8)
        for c in range(8):
            rows[c, pl.ds(at, 8), :] = v[8 * c:8 * c + 8]
        return 0
    lax.fori_loop(0, 32, one, 0)


def flip(eye, rows_c):
    return lax.dot_general(eye, rows_c.astype(jnp.bfloat16), NT, preferred_element_type=jnp.float32)


def proof_kernel(recv, eye, out, power, stage, rows, mat_re, mat_im, sem):
    cp = pltpu.make_async_copy(recv.at[0], stage, sem)
    cp.start()
    cp.wait()
    gather_rows(stage, rows)
    for w in range(8):
        r = rows[w]
        power[w:w + 1, :] = jnp.sum(r * r, axis=0, keepdims=True)
        t = flip(eye[...], r)
        mat_re[pl.ds(w, 256, stride=8), :] = t[:, :128]
        mat_im[pl.ds(w, 256, stride=8), :] = t[:, 128:]

    def one(f, _):
        at = pl.ds(pl.multiple_of(f * 8, 8), 8)
        out[f] = jnp.concatenate([mat_re[at, :], mat_im[at, :]], axis=1).astype(jnp.bfloat16)
        return 0
    lax.fori_loop(0, 256, one, 0)


def proof_matrix(recv, eye):
    vm = pl.BlockSpec(memory_space=pltpu.VMEM)
    return pl.pallas_call(
        proof_kernel,
        out_shape=(jax.ShapeDtypeStruct((256, 8, 256), jnp.bfloat16),
                   jax.ShapeDtypeStruct((8, 256), jnp.float32)),
        in_specs=[pl.BlockSpec(memory_space=pl.ANY), vm],
        out_specs=(vm, vm),
        scratch_shapes=[
            pltpu.VMEM((16, 2, 64, 256), jnp.bfloat16),
            pltpu.VMEM((8, 256, 256), jnp.float32),
            pltpu.VMEM((256 * 8, 128), jnp.float32),
            pltpu.VMEM((256 * 8, 128), jnp.float32),
            pltpu.SemaphoreType.DMA,
        ],
        compiler_params=pltpu.CompilerParams(vmem_limit_bytes=62 * 2 ** 20),
    )(recv, eye)


def coherence_kernel(recv, wmat, wpow, eye, out, stage, rows, mat_re, mat_im, wv, apow, tile, load_sem, w_sem, out_sem):
    wcp = pltpu.make_async_copy(wmat, wv, w_sem)
    wcp.start()

    def load(b):
        return pltpu.make_async_copy(recv.at[b + 1], stage.at[lax.rem(b, 2)], load_sem.at[lax.rem(b, 2)])

    load(0).start()

    def block(b, _):
        @pl.when(b < 7)
        def _():
            load(b + 1).start()
        load(b).wait()
        gather_rows(stage.at[lax.rem(b, 2)], rows)
        e = eye[...]
        for c in range(8):
            r = rows[c]
            apow[b, c:c + 1, :] = jnp.sum(r * r, axis=0, keepdims=True)
            t = flip(e, r)
            mat_re[pl.ds(b * 8 + c, 256, stride=PITCH), :] = t[:, :128]
            mat_im[pl.ds(b * 8 + c, 256, stride=PITCH), :] = t[:, 128:]
        return 0

    lax.fori_loop(0, 8, block, 0)
    wcp.wait()

    def bins(i, _):
        for u in range(8):
            f = i * 8 + u
            at = pl.ds(pl.multiple_of(f * PITCH, 8), 64)
            are, aim = mat_re[at, :], mat_im[at, :]
            left = jnp.concatenate([
                jnp.concatenate([are, aim], axis=1),
                jnp.concatenate([aim, -are], axis=1)], axis=0).astype(jnp.bfloat16)
            g = lax.dot_general(left, wv[f], NT, preferred_element_type=jnp.float32)
            mat_re[at, 0:64] = g[:64] * g[:64] + g[64:] * g[64:]
        return 0

    lax.fori_loop(0, 32, bins, 0)

    def store(b):
        return pltpu.make_async_copy(tile.at[lax.rem(b, 2)], out.at[pl.ds(b * 8, 8)], out_sem.at[lax.rem(b, 2)])

    def finish(b, _):
        @pl.when(b >= 2)
        def _():
            store(b - 2).wait()
        for c in range(8):
            for h in range(2):
                num = mat_re[pl.ds(h * 128 * PITCH + b * 8 + c, 128, stride=PITCH), :].T
                cols = slice(128 * h, 128 * h + 128)
                den = (apow[b, c:c + 1, cols] + 1e-06) * (wpow[:, cols] + 1e-06)
                tile[lax.rem(b, 2), c, :, cols] = num[:64] / den
        store(b).start()
        return 0

    lax.fori_loop(0, 8, finish, 0)
    store(6).wait()
    store(7).wait()


def coherence(recv, wmat, wpow, eye):
    vm = pl.BlockSpec(memory_space=pltpu.VMEM)
    hbm = pl.BlockSpec(memory_space=pl.ANY)
    dma = pltpu.SemaphoreType.DMA
    return pl.pallas_call(
        coherence_kernel,
        out_shape=jax.ShapeDtypeStruct((64, 64, 256), jnp.float32),
        in_specs=[hbm, hbm, vm, vm],
        out_specs=hbm,
        scratch_shapes=[
            pltpu.VMEM((2, 16, 2, 64, 256), jnp.bfloat16),
            pltpu.VMEM((8, 256, 256), jnp.float32),
            pltpu.VMEM((256 * PITCH, 128), jnp.float32),
            pltpu.VMEM((256 * PITCH, 128), jnp.float32),
            pltpu.VMEM((256, 64, 256), jnp.bfloat16),
            pltpu.VMEM((8, 8, 256), jnp.float32),
            pltpu.VMEM((2, 8, 64, 256), jnp.float32),
            dma((2,)), dma, dma((2,)),
        ],
        compiler_params=pltpu.CompilerParams(vmem_limit_bytes=62 * 2 ** 20),
    )(recv, wmat, wpow, eye)


def tiles(a):
    return a.reshape(a.shape[0] // 8, 8, 256, 128).transpose(0, 2, 1, 3)


def per_device(auxiliary, proofs):
    peers = lax.axis_size("tm")
    recv = spectra(tiles(auxiliary), tiles(proofs), peers)
    eye = jnp.eye(256, dtype=jnp.bfloat16)
    wpart, wpow = proof_matrix(recv, eye)
    wmat = lax.all_gather(wpart, "chan", axis=1, tiled=True)
    wpow = lax.all_gather(wpow, "chan", axis=0, tiled=True)
    return coherence(recv, wmat, wpow, eye)


def solution(mesh):
    return jax.shard_map(
        per_device,
        mesh=mesh,
        in_specs=(P("chan", "tm"), P("chan", "tm")),
        out_specs=P("chan", None, "tm"),
        check_vma=False,
    )
```

time: 853 us -> 307 us (0.36)
  matrix products: 300 us -> 0 us
  local copies, waits for them, and re-layouts: 276 us -> 0 us
  Pallas kernels: 0 us -> 174 us
  blocking collectives: 174 us -> 31.1 us
  waiting for transfers between devices: 0.02 us -> 86.9 us
  other arithmetic: 59.1 us -> 0.67 us
  loops' own time: 15.5 us -> 0 us
    dot_general x56 -> x0, matrix products: 300 us -> none  [the longest x9 71.1 us: transform_block(): jnp.einsum('rkq,qm->rmk', imag_two, cos_second, precision=highest)]
    pallas_call x0 -> x3, Pallas kernels: none -> 174 us  [the longest x1 140 us: spectra(): pl.pallas_call(functools.partial(spectra_kernel, peers), out_shape=jax.Sh...]
    all_to_all x2 -> x0, blocking collectives: 146 us -> none  [the longest x1 122 us: per_device(): lax.all_to_all(aux_spec, 'tm', split_axis=3, concat_axis=2, tiled=True)]
    unnamed x15 -> x0, local copies, waits for them, and re-layouts: 95.7 us -> none
    all_gather x1, waiting for transfers between devices: 0.01 us -> 86.9 us  [per_device(): wmat = lax.all_gather(wpart, 'chan', axis=1, tiled=True)]
    slice x6 -> x0, local copies, waits for them, and re-layouts: 53.7 us -> none  [the longest x1 24.6 us: per_device(): aux_spec = spectra[:, :aux_rows]]
    all_to_all x2 -> x0, local copies, waits for them, and re-layouts: 38.7 us -> none  [the longest x1 22.7 us: per_device(): lax.all_to_all(aux_spec, 'tm', split_axis=3, concat_axis=2, tiled=True)]
    all_gather x0 -> x1, blocking collectives: none -> 31.1 us  [per_device(): wpow = lax.all_gather(wpow, 'chan', axis=0, tiled=True)]
  transfers between devices with their start and end apart: 3 -> 1, of which waited for: 0 -> 1; matrix products, arithmetic and copies ran while one was open for 15% -> 0% of each run, Pallas kernels for 0% -> 0%
where the time goes in v1:
time: 307 us; the launch traced here: 306 us
  Pallas kernels  174 us (57%)
  waiting for transfers between devices  86.9 us (28%)
  blocking collectives  31.1 us (10%)
  between operations  13.4 us (4%)
    pallas_call x1, Pallas kernels, spectra(): pl.pallas_call(functools.partial(spectra_kernel, peers), out_shape=jax.Sh...  140 us
    all_gather x1, waiting for transfers between devices, per_device(): wmat = lax.all_gather(wpart, 'chan', axis=1, tiled=True)  86.9 us
    all_gather x1, blocking collectives, per_device(): wpow = lax.all_gather(wpow, 'chan', axis=0, tiled=True)  31.1 us
    pallas_call x1, Pallas kernels, coherence(): pl.pallas_call(coherence_kernel, out_shape=jax.ShapeDtypeStruct((64, 64,...  27.7 us
  transfers between devices with their start and end apart: 1, of which 1 were waited for; matrix products, arithmetic and copies ran while one was open for 0% of the time, Pallas kernels for 0%

profile of v1, /device:TPU:1, one launch (start us, length us, event | category | flops | bytes accessed | tf_op | source)
XLA Modules:
  0.0 305.9 jit_solution(7471582512126101733)
XLA Ops:
  6.5 0.0 all-gather.2.cloned.1.call-start
  6.5 0.7 fusion.eye
  7.2 140.3 %shard_map.73.recv = bf16[9,16,2,64,256]{4,3,2,1,0:T(8,128)(2,1)} custom-call(f32[8,256,8,128]{3,2,1,0:T(8,128)} %bitcast.6, f32[1,256,8,128]{3,2,1,0:T(8,128)} %bitcast.7, bf16[128,256]{1,0:T(8,128)(2,1)} %constant.19.f1, bf16[128,256]{1,0:T(8,128)(2,1)} %constant.24.w2, f32[128,128]{1,0:T(8,128)} %constant.12.clone.cos_t, ...), custom_call_target="tpu_custom_call" | custom-call | tf_op jit(solution)/shard_map/pallas_call | solution.py:216
  147.5 5.8 %shard_map.74 = (bf16[256,8,256]{2,1,0:T(8,128)(2,1)}, f32[8,256]{1,0:T(8,128)}) custom-call(bf16[9,16,2,64,256]{4,3,2,1,0:T(8,128)(2,1)} %shard_map.73.recv, bf16[256,256]{1,0:T(8,128)(2,1)} %fusion.eye), custom_call_target="tpu_custom_call" | custom-call | tf_op jit(solution)/shard_map/pallas_call | solution.py:273
  153.3 0.0 all-gather.2.cloned.1.call-update
  153.3 31.1 %all_gather.7.wpow = f32[64,256]{1,0:T(8,128)} all-gather(f32[8,256]{1,0:T(8,128)} %get-tuple-element.8), channel_id=1, replica_groups=mesh['tm'=16,'chan'=8] {'chan'}, dimensions={0}, use_global_device_ids=true | all-gather | bytes 73728 | tf_op jit(solution)/shard_map/all_gather | solution.py:385
  184.4 86.9 %all-gather.2.cloned.1.call-done.wmat = bf16[256,64,256]{2,1,0:T(8,128)(2,1)} async-done(((bf16[256,8,256]{2,1,0:T(8,128)(2,1)}), bf16[256,64,256]{2,1,0:T(8,128)(2,1)}) %all-gather.2.cloned.1.call-update) | async-done | bytes 8388624 | tf_op jit(solution)/shard_map/all_gather | solution.py:384
  271.3 27.7 %shard_map.75 = f32[64,64,256]{2,1,0:T(8,128)} custom-call(bf16[9,16,2,64,256]{4,3,2,1,0:T(8,128)(2,1)} %shard_map.73.recv, bf16[256,64,256]{2,1,0:T(8,128)(2,1)} %all-gather.2.cloned.1.call-done.wmat, f32[64,256]{1,0:T(8,128)} %all_gather.7.wpow, bf16[256,256]{1,0:T(8,128)(2,1)} %fusion.eye), custom_call_target="tpu_custom_call" | custom-call | tf_op jit(solution)/shard_map/pallas_call | solution.py:356
Async XLA Ops:
  6.5 264.8 %all-gather.2.cloned.1.call-start = ((), (), s32[]{:S(2)}) async-start(), calls=%async_computation | async-start | bytes 9437184 | tf_op jit(solution)/shard_map/all_gather | solution.py:384
Sparse Core Ops, SparseCore 0:
  153.5 117.8 all-gather.1

commit v2 on v1

v2 whole, which is shorter than its diff:
```python
import math
import functools
import numpy as np
import jax
import jax.numpy as jnp
from jax import lax
from jax.sharding import PartitionSpec as P
from jax.experimental import pallas as pl
from jax.experimental.pallas import tpu as pltpu

NT = (((1,), (1,)), ((), ()))
PITCH = 72


def split(x):
    hi = x.astype(jnp.bfloat16)
    lo = (x - hi.astype(jnp.float32)).astype(jnp.bfloat16)
    return hi, lo


def np_split(x):
    x = jnp.asarray(x, jnp.float32)
    return split(x)


def fft_tables():
    a = np.arange(64)
    ang = 2 * np.pi * np.outer(a, a) % (2 * np.pi * 64) / 64
    ang = 2 * np.pi * (np.outer(a, a) % 64) / 64
    f1 = np.concatenate([np.cos(ang), -np.sin(ang)], 0)
    h, l = np_split(f1)
    f1cat = jnp.concatenate([h, h, l, l], axis=1)
    lane = np.arange(128)
    k2 = np.arange(32)
    ang2 = 2 * np.pi * (np.outer(k2, lane) % 64) / 64
    re = np.concatenate([np.cos(ang2), np.sin(ang2)], 1)
    im = np.concatenate([-np.sin(ang2), np.cos(ang2)], 1)
    h, l = np_split(np.concatenate([re, im], 0))
    w2 = jnp.concatenate([h, l], axis=0)
    k1 = np.arange(128)
    angt = 2 * np.pi * (np.outer(k1, lane) % 8192) / 8192
    cos_t = jnp.asarray(np.cos(angt), jnp.float32)
    sin_t = jnp.asarray(np.sin(angt), jnp.float32)
    n = np.arange(8192)
    hann = jnp.asarray((0.5 - 0.5 * np.cos(2 * np.pi * n / 8192)).reshape(64, 128), jnp.float32)
    return f1cat, w2, cos_t, sin_t, hann


def fft_step(x2d, base, mean8, scr, s, tabs):
    f1, w2, cos_t, sin_t, hann = tabs
    cats = []
    for c in range(8):
        xs = (x2d[pl.ds(base + s * 256 + c, 64, stride=8), :] - mean8[c:c + 1]) * hann[...]
        h, l = split(xs)
        cats.append(jnp.concatenate([h, l, h, l], axis=0))
    y = jnp.dot(f1[...], jnp.concatenate(cats, axis=1), preferred_element_type=jnp.float32)
    zh, zl = [], []
    for c in range(8):
        yre = y[:64, 128 * c:128 * c + 128]
        yim = y[64:, 128 * c:128 * c + 128]
        for b in range(2):
            ct = cos_t[64 * b:64 * b + 64]
            st = sin_t[64 * b:64 * b + 64]
            h, l = split(jnp.concatenate([yre * ct + yim * st, yim * ct - yre * st], axis=1))
            zh.append(h)
            zl.append(l)
    w = w2[...]
    a = lax.dot_general(w, jnp.concatenate(zh, axis=0), NT, preferred_element_type=jnp.float32)
    b = lax.dot_general(w[:64], jnp.concatenate(zl, axis=0), NT, preferred_element_type=jnp.float32)
    o = a[:64] + a[64:] + b
    for c in range(8):
        scr[pl.ds(c * 8 + s, 64, stride=PITCH), :] = o[:, 128 * c:128 * c + 128]


def fused_kernel(peers, aux, wit, eye, f1, w2, cos_t, sin_t, hann, num, apow, wpow,
                 x, scr, send, recv, sums, means, rows, mat_re, mat_im, wv, tile,
                 load_sem, halo_send, halo_recv, sum_send, sum_recv, send_sem, recv_sem,
                 ring_send, ring_recv, out_sem):
    tabs = (f1, w2, cos_t, sin_t, hann)
    mesh_id = pl.DeviceIdType.MESH
    me = lax.axis_index("tm")
    mine = lax.axis_index("chan")
    across = mine + 1 - 2 * lax.rem(mine, 2)
    right = lax.rem(mine + 2, 8)
    left = lax.rem(mine + 6, 8)
    before = lax.rem(me + peers - 1, peers)
    blocks = x.shape[0]
    slots = send.shape[0]

    def source(b):
        return wit.at[0] if b == 0 else aux.at[b - 1]

    loads = []
    for b in range(blocks):
        cp = pltpu.make_async_copy(source(b), x.at[b, pl.ds(0, 256)], load_sem.at[b])
        cp.start()
        loads.append(cp)
    barrier = pltpu.get_barrier_semaphore()

    def greet(j, _):
        pl.semaphore_signal(barrier, inc=1, device_id={"tm": lax.rem(me + j, peers)}, device_id_type=mesh_id)
        return 0

    lax.fori_loop(1, peers, greet, 0)
    for c in (across, right, left):
        pl.semaphore_signal(barrier, inc=1, device_id={"chan": c}, device_id_type=mesh_id)
    pl.semaphore_wait(barrier, peers + 2)

    halos = []
    for b in range(blocks):
        cp = pltpu.make_async_remote_copy(
            src_ref=source(b).at[pl.ds(0, 32)], dst_ref=x.at[b, pl.ds(256, 32)],
            send_sem=halo_send.at[b], recv_sem=halo_recv.at[b],
            device_id={"tm": before}, device_id_type=mesh_id)
        cp.start()
        halos.append(cp)

    lane = lax.broadcasted_iota(jnp.int32, (8, 128), 1)
    total = jnp.zeros((8, 128), jnp.float32)
    for b in range(blocks):
        loads[b].wait()

        def add(i, acc):
            return acc + jnp.sum(x[b, pl.ds(i * 16, 16)], axis=0)

        part = lax.fori_loop(0, 16, add, jnp.zeros((8, 128), jnp.float32))
        total = jnp.where(lane == b, jnp.sum(part, axis=1, keepdims=True), total)
    sums[0] = total

    def sum_copy(j):
        return pltpu.make_async_remote_copy(
            src_ref=sums.at[0], dst_ref=sums.at[j], send_sem=sum_send.at[j], recv_sem=sum_recv.at[j],
            device_id={"tm": lax.rem(me + j, peers)}, device_id_type=mesh_id)

    def sum_start(j, _):
        sum_copy(j).start()
        return 0

    def sum_wait(j, acc):
        sum_copy(j).wait()
        return acc + sums[j]

    lax.fori_loop(1, peers, sum_start, 0)
    total = lax.fori_loop(1, peers, sum_wait, total)
    mean = total / (256 * 128 * peers)
    for b in range(blocks):
        means[b] = jnp.broadcast_to(mean[:, b:b + 1], (8, 128))
    for b in range(blocks):
        halos[b].wait()

    x2d = x.reshape(blocks * 288 * 8, 128)
    row = lax.broadcasted_iota(jnp.int32, (64, 128), 0)
    keep = jnp.where((lax.rem(row, 8) == 7) & (me == peers - 1), 0.0, 1.0)

    def block_copy(b, j):
        slot = lax.rem(b, slots)
        to = lax.rem(me + j, peers)
        return pltpu.make_async_remote_copy(
            src_ref=send.at[slot, to], dst_ref=recv.at[b, me],
            send_sem=send_sem.at[slot, j], recv_sem=recv_sem.at[b, j],
            device_id={"tm": to}, device_id_type=mesh_id)

    def drain(b):
        def one(j, _):
            block_copy(b, j).wait_send()
            return 0
        lax.fori_loop(1, peers, one, 0)

    def landed(b):
        def one(j, _):
            block_copy(b, j).wait_recv()
            return 0
        lax.fori_loop(1, peers, one, 0)

    def piece(i, g, lo, n, c):
        return pltpu.make_async_remote_copy(
            src_ref=wv.at[g, pl.ds(lo, n)], dst_ref=wv.at[g, pl.ds(lo, n)],
            send_sem=ring_send.at[i], recv_sem=ring_recv.at[i],
            device_id={"chan": c}, device_id_type=mesh_id)

    frames = wv.shape[1]
    half = frames // 2
    zx = piece(0, mine, 0, frames, across)
    own_r = piece(1, mine, 0, frames, right)
    own_l = piece(2, mine, 0, frames, left)
    far_r = piece(3, across, 0, frames, right)
    far_l = piece(4, across, 0, frames, left)
    left_across = lax.rem(across + 6, 8)
    right_across = lax.rem(across + 2, 8)
    own_rr = piece(5, left, 0, half, right)
    own_ll = piece(6, right, half, half, left)
    far_rr = piece(7, left_across, 0, half, right)
    far_ll = piece(8, right_across, half, half, left)

    def proof_block():
        landed(0)
        gather_rows(recv.at[0], rows)
        power = []
        for w in range(8):
            r = rows[w]
            power.append(jnp.sum(r * r, axis=0, keepdims=True))
            t = flip(eye[...], r)
            mat_re[pl.ds(w, 256, stride=16), :] = t[:, :128]
            mat_re[pl.ds(8 + w, 256, stride=16), :] = t[:, 128:]

        def one(f, _):
            wv[mine, f] = mat_re[pl.ds(pl.multiple_of(f * 16, 16), 16), :].astype(jnp.bfloat16)
            return 0
        lax.fori_loop(0, 256, one, 0)
        rest = jnp.concatenate(power, axis=0)
        zero = jnp.zeros((8, 128), jnp.float32)
        for term in range(3):
            top = rest.astype(jnp.bfloat16).astype(jnp.float32)
            for h in range(2):
                wv[mine, 256 + 3 * h + term] = jnp.concatenate(
                    [top[:, 128 * h:128 * h + 128], zero], axis=0).astype(jnp.bfloat16)
            rest = rest - top
        for i in range(262, frames):
            wv[mine, i] = jnp.zeros((16, 128), jnp.bfloat16)
        zx.start()
        own_r.start()
        own_l.start()

    def aux_block(b):
        landed(b)
        gather_rows(recv.at[b], rows)
        e = eye[...]
        for c in range(8):
            r = rows[c]
            apow[b - 1, c:c + 1, :] = jnp.sum(r * r, axis=0, keepdims=True)
            t = flip(e, r)
            at = (b - 1) * 8 + c
            mat_re[pl.ds(at, 256, stride=PITCH), :] = t[:, :128]
            mat_im[pl.ds(at, 256, stride=PITCH), :] = t[:, 128:]

    def block(b, _):
        slot = lax.rem(b, slots)
        mean8 = means[b]

        def step(s, _):
            fft_step(x2d, b * 2304, mean8, scr, s, tabs)
            return 0

        lax.fori_loop(0, 8, step, 0)

        @pl.when(b >= slots)
        def _():
            drain(b - slots)

        def pack(d, _):
            for part in range(2):
                for hf in range(2):
                    at = pl.multiple_of((part * 32 + d * 2 + hf) * PITCH, 8)
                    v = scr[pl.ds(at, 64), :] * keep
                    send[slot, d, part, :, hf * 128:hf * 128 + 128] = v.astype(jnp.bfloat16)
            return 0

        lax.fori_loop(0, peers, pack, 0)

        def go(j, _):
            block_copy(b, j).start()
            return 0

        lax.fori_loop(1, peers, go, 0)
        recv[b, me] = send[slot, me]

        @pl.when(b == 1)
        def _():
            proof_block()

        @pl.when(b >= 3)
        def _():
            aux_block(b - 2)

        @pl.when(b == 4)
        def _():
            zx.wait_recv()
            far_r.start()
            far_l.start()

        @pl.when(b == 5)
        def _():
            own_r.wait_recv()
            own_l.wait_recv()
            own_rr.start()
            own_ll.start()

        @pl.when(b == 7)
        def _():
            far_r.wait_recv()
            far_l.wait_recv()
            far_rr.start()
            far_ll.start()
        return 0

    lax.fori_loop(0, blocks, block, 0)

    def store(b):
        return pltpu.make_async_copy(tile.at[lax.rem(b, 2)], num.at[pl.ds(b * 8, 8)], out_sem.at[lax.rem(b, 2)])

    def finish(b0, nb):
        n = nb * 8

        def bins(i, _):
            for u in range(8):
                f = i * 8 + u
                at = pl.ds(pl.multiple_of(f * PITCH + b0 * 8, 8), n)
                lhs = jnp.concatenate([mat_re[at, :], mat_im[at, :]], axis=0).astype(jnp.bfloat16)
                g = lax.dot_general(lhs, wv[:, f].reshape(128, 128), NT, preferred_element_type=jnp.float32)
                p, q = g[:n], g[n:]
                re = p + pltpu.roll(q, 120, 1)
                im = q - pltpu.roll(p, 120, 1)
                mat_re[at, :] = re * re + im * im
            return 0

        lax.fori_loop(0, 32, bins, 0)

        def emit(b, _):
            @pl.when(b >= 2)
            def _():
                store(b - 2).wait()
            for c in range(8):
                for h in range(2):
                    t = mat_re[pl.ds(h * 128 * PITCH + b * 8 + c, 128, stride=PITCH), :].T
                    for g in range(8):
                        tile[lax.rem(b, 2), c, 8 * g:8 * g + 8, 128 * h:128 * h + 128] = t[16 * g:16 * g + 8]
            store(b).start()
            return 0

        lax.fori_loop(b0, b0 + nb, emit, 0)

    own_rr.wait_recv()
    own_ll.wait_recv()
    far_rr.wait_recv()
    far_ll.wait_recv()
    finish(0, 4)
    aux_block(7)
    aux_block(8)
    finish(4, 4)
    for h in range(2):
        for g in range(8):
            v = [wv[g, 256 + 3 * h + term].astype(jnp.float32)[:8] for term in range(3)]
            wpow[8 * g:8 * g + 8, 128 * h:128 * h + 128] = v[0] + v[1] + v[2]
    for cp in (zx, own_r, own_l, far_r, far_l, own_rr, own_ll, far_rr, far_ll):
        cp.wait_send()
    for b in range(blocks - slots, blocks):
        drain(b)
    store(6).wait()
    store(7).wait()


def gather_rows(stage, rows):
    def one(t, _):
        for part in range(2):
            v = stage[t, part].astype(jnp.float32)
            at = pl.multiple_of(part * 128 + t * 8, 8)
            for c in range(8):
                rows[c, pl.ds(at, 8), :] = v[8 * c:8 * c + 8]
        return 0
    lax.fori_loop(0, 16, one, 0)


def flip(eye, rows_c):
    return lax.dot_general(eye, rows_c.astype(jnp.bfloat16), NT, preferred_element_type=jnp.float32)


def fused(aux, wit, peers):
    tabs = fft_tables()
    eye = jnp.eye(256, dtype=jnp.bfloat16)
    vm = pl.BlockSpec(memory_space=pltpu.VMEM)
    hbm = pl.BlockSpec(memory_space=pl.ANY)
    blocks = aux.shape[0] + 1
    slots = 3
    dma = pltpu.SemaphoreType.DMA
    f32, bf16 = jnp.float32, jnp.bfloat16
    return pl.pallas_call(
        functools.partial(fused_kernel, peers),
        out_shape=(jax.ShapeDtypeStruct((64, 64, 256), f32),
                   jax.ShapeDtypeStruct((8, 8, 256), f32),
                   jax.ShapeDtypeStruct((64, 256), f32)),
        in_specs=[hbm, hbm] + [vm] * 6,
        out_specs=(hbm, vm, vm),
        scratch_shapes=[
            pltpu.VMEM((blocks, 288, 8, 128), f32),
            pltpu.VMEM((64 * PITCH, 128), f32),
            pltpu.VMEM((slots, peers, 2, 64, 256), bf16),
            pltpu.VMEM((blocks, peers, 2, 64, 256), bf16),
            pltpu.VMEM((peers, 8, 128), f32),
            pltpu.VMEM((blocks, 8, 128), f32),
            pltpu.VMEM((8, 256, 256), f32),
            pltpu.VMEM((256 * PITCH, 128), f32),
            pltpu.VMEM((256 * PITCH, 128), f32),
            pltpu.VMEM((8, 264, 16, 128), bf16),
            pltpu.VMEM((2, 8, 64, 256), f32),
            dma((blocks,)), dma((blocks,)), dma((blocks,)),
            dma((peers,)), dma((peers,)),
            dma((slots, peers)), dma((blocks, peers)),
            dma((9,)), dma((9,)), dma((2,)),
        ],
        compiler_params=pltpu.CompilerParams(
            collective_id=0, has_side_effects=True, vmem_limit_bytes=63 * 2 ** 20),
    )(aux, wit, eye, *tabs)


def tiles(a):
    return a.reshape(a.shape[0] // 8, 8, 256, 128).transpose(0, 2, 1, 3)


def per_device(auxiliary, proofs):
    peers = lax.axis_size("tm")
    num, apow, wpow = fused(tiles(auxiliary), tiles(proofs), peers)
    apow = apow.reshape(64, 256)
    return num / ((apow[:, None, :] + 1e-06) * (wpow[None, :, :] + 1e-06))


def solution(mesh):
    return jax.shard_map(
        per_device,
        mesh=mesh,
        in_specs=(P("chan", "tm"), P("chan", "tm")),
        out_specs=P("chan", None, "tm"),
        check_vma=False,
    )
```

time: 307 us -> 198 us (0.64)
  waiting for transfers between devices: 86.9 us -> 0 us
  blocking collectives: 31.1 us -> 0 us
  Pallas kernels: 174 us -> 188 us
  between operations: 13.4 us -> 0.01 us
  other arithmetic: 0.67 us -> 7.52 us
    all_gather x1 -> x0, waiting for transfers between devices: 86.9 us -> none  [per_device(): wmat = lax.all_gather(wpart, 'chan', axis=1, tiled=True)]
    all_gather x1 -> x0, blocking collectives: 31.1 us -> none  [per_device(): wpow = lax.all_gather(wpow, 'chan', axis=0, tiled=True)]
    pallas_call x3 -> x1, Pallas kernels: 174 us -> 188 us  [fused(): pl.pallas_call(functools.partial(fused_kernel, peers), out_shape=(jax.Sha...]
    div x0 -> x1, other arithmetic: none -> 5.15 us  [per_device(): return num / ((apow[:, None, :] + 1e-06) * (wpow[None, :, :] + 1e-06))]
  transfers between devices with their start and end apart: 1 -> 0, of which waited for: 1 -> 0; matrix products, arithmetic and copies ran while one was open for 0% -> 0% of each run, Pallas kernels for 0% -> 0%
where the time goes in v2:
time: 198 us; the launch traced here: 195 us
  Pallas kernels  188 us (95%)
  other arithmetic  7.52 us (4%)
    pallas_call x1, Pallas kernels, fused(): pl.pallas_call(functools.partial(fused_kernel, peers), out_shape=(jax.Sha...  188 us
    div x1, other arithmetic, per_device(): return num / ((apow[:, None, :] + 1e-06) * (wpow[None, :, :] + 1e-06))  5.15 us

profile of v2, /device:TPU:1, one launch (start us, length us, event | category | flops | bytes accessed | tf_op | source)
XLA Modules:
  0.0 195.4 jit_solution(14092996015010992055)
XLA Ops:
  0.0 0.7 fusion.eye
  0.7 187.9 %shard_map.73 = (f32[64,64,256]{2,1,0:T(8,128)}, f32[8,8,256]{2,1,0:T(8,128)}, f32[64,256]{1,0:T(8,128)}) custom-call(f32[8,256,8,128]{3,2,1,0:T(8,128)} %bitcast.8, f32[1,256,8,128]{3,2,1,0:T(8,128)} %bitcast.9, bf16[256,256]{1,0:T(8,128)(2,1)} %fusion.eye, bf16[128,256]{1,0:T(8,128)(2,1)} %constant.22.f1, bf16[128,256]{1,0:T(8,128)(2,1)} %constant.27.w2, ...), custom_call_target="tpu_custom_call" | custom-call | tf_op jit(solution)/shard_map/pallas_call | solution.py:376
  188.6 0.8 add_bitcast_fusion
  189.4 0.8 broadcast_add_fusion
  190.3 5.2 %multiply_divide_fusion = f32[64,64,256]{2,1,0:T(8,128)} fusion(f32[64,64,256]{2,1,0:T(8,128)} %get-tuple-element.8, f32[64,256]{1,0:T(8,128)S(1)} %broadcast_add_fusion, f32[64,256]{1,0:T(8,128)S(1)} %add_bitcast_fusion), kind=kLoop, calls=%fused_computation | loop fusion | flops 2097152 | bytes 8519680 | tf_op jit(solution)/shard_map/div | solution.py:413

commit v3 on v2

--- a/solution.py
+++ b/solution.py
@@ -73,9 +73,9 @@
 
 
 def fused_kernel(peers, aux, wit, eye, f1, w2, cos_t, sin_t, hann, num, apow, wpow,
-                 x, scr, send, recv, sums, means, rows, mat_re, mat_im, wv, tile,
+                 x, scr, send, recv, sums, means, diffs, rows, mat_re, mat_im, wv, tile,
                  load_sem, halo_send, halo_recv, sum_send, sum_recv, send_sem, recv_sem,
-                 ring_send, ring_recv, out_sem):
+                 cross_send, cross_recv, ring_send, ring_recv, out_sem):
     tabs = (f1, w2, cos_t, sin_t, hann)
     mesh_id = pl.DeviceIdType.MESH
     me = lax.axis_index("tm")
@@ -90,42 +90,47 @@
     def source(b):
         return wit.at[0] if b == 0 else aux.at[b - 1]
 
+    barrier = pltpu.get_barrier_semaphore()
+
+    def greet(j, _):
+        to = lax.rem(me + j, peers)
+        pl.semaphore_signal(barrier, inc=1, device_id={"tm": to}, device_id_type=mesh_id)
+        pl.semaphore_signal(barrier, inc=1, device_id={"tm": to, "chan": across}, device_id_type=mesh_id)
+        return 0
+
+    lax.fori_loop(1, peers, greet, 0)
+    for c in (across, right, left):
+        pl.semaphore_signal(barrier, inc=1, device_id={"chan": c}, device_id_type=mesh_id)
     loads = []
     for b in range(blocks):
         cp = pltpu.make_async_copy(source(b), x.at[b, pl.ds(0, 256)], load_sem.at[b])
         cp.start()
         loads.append(cp)
-    barrier = pltpu.get_barrier_semaphore()
-
-    def greet(j, _):
-        pl.semaphore_signal(barrier, inc=1, device_id={"tm": lax.rem(me + j, peers)}, device_id_type=mesh_id)
-        return 0
-
-    lax.fori_loop(1, peers, greet, 0)
-    for c in (across, right, left):
-        pl.semaphore_signal(barrier, inc=1, device_id={"chan": c}, device_id_type=mesh_id)
-    pl.semaphore_wait(barrier, peers + 2)
-
-    halos = []
-    for b in range(blocks):
-        cp = pltpu.make_async_remote_copy(
-            src_ref=source(b).at[pl.ds(0, 32)], dst_ref=x.at[b, pl.ds(256, 32)],
+    pl.semaphore_wait(barrier, 2 * (peers - 1) + 3)
+
+    def halo(b, src):
+        return pltpu.make_async_remote_copy(
+            src_ref=src.at[pl.ds(0, 32)], dst_ref=x.at[b, pl.ds(256, 32)],
             send_sem=halo_send.at[b], recv_sem=halo_recv.at[b],
             device_id={"tm": before}, device_id_type=mesh_id)
-        cp.start()
-        halos.append(cp)
+
+    for b in range(blocks):
+        halo(b, source(b)).start()
 
     lane = lax.broadcasted_iota(jnp.int32, (8, 128), 1)
-    total = jnp.zeros((8, 128), jnp.float32)
+    local = jnp.zeros((8, 128), jnp.float32)
     for b in range(blocks):
         loads[b].wait()
 
         def add(i, acc):
-            return acc + jnp.sum(x[b, pl.ds(i * 16, 16)], axis=0)
-
-        part = lax.fori_loop(0, 16, add, jnp.zeros((8, 128), jnp.float32))
-        total = jnp.where(lane == b, jnp.sum(part, axis=1, keepdims=True), total)
-    sums[0] = total
+            return acc + jnp.sum(x[b, pl.ds(i * 32, 32)].reshape(8, 4, 8, 128), axis=0)
+
+        part = jnp.sum(lax.fori_loop(0, 8, add, jnp.zeros((4, 8, 128), jnp.float32)), axis=0)
+        local = jnp.where(lane == b, jnp.sum(part, axis=1, keepdims=True), local)
+    sums[0] = local
+    local_mean = local / (256 * 128)
+    for b in range(blocks):
+        means[b] = jnp.broadcast_to(local_mean[:, b:b + 1], (8, 128))
 
     def sum_copy(j):
         return pltpu.make_async_remote_copy(
@@ -141,20 +146,22 @@
         return acc + sums[j]
 
     lax.fori_loop(1, peers, sum_start, 0)
-    total = lax.fori_loop(1, peers, sum_wait, total)
-    mean = total / (256 * 128 * peers)
-    for b in range(blocks):
-        means[b] = jnp.broadcast_to(mean[:, b:b + 1], (8, 128))
-    for b in range(blocks):
-        halos[b].wait()
+
+    def total_means():
+        total = lax.fori_loop(1, peers, sum_wait, sums[0])
+        mean = total / (256 * 128 * peers)
+        for b in range(blocks):
+            diffs[b] = means[b] - jnp.broadcast_to(mean[:, b:b + 1], (8, 128))
 
     x2d = x.reshape(blocks * 288 * 8, 128)
     row = lax.broadcasted_iota(jnp.int32, (64, 128), 0)
     keep = jnp.where((lax.rem(row, 8) == 7) & (me == peers - 1), 0.0, 1.0)
+    col = lax.broadcasted_iota(jnp.int32, (64, 128), 1)
+    hann_bins = jnp.where(col == 0, 4096.0, jnp.where(col == 1, -2048.0, 0.0))
 
     def block_copy(b, j):
         slot = lax.rem(b, slots)
-        to = lax.rem(me + j, peers)
+        to = lax.rem(me + 7 * j, peers)
         return pltpu.make_async_remote_copy(
             src_ref=send.at[slot, to], dst_ref=recv.at[b, me],
             send_sem=send_sem.at[slot, j], recv_sem=recv_sem.at[b, j],
@@ -165,6 +172,13 @@
             block_copy(b, j).wait_send()
             return 0
         lax.fori_loop(1, peers, one, 0)
+
+    def cross_copy(j):
+        to = lax.rem(me + 7 * j, peers)
+        return pltpu.make_async_remote_copy(
+            src_ref=send.at[0, to], dst_ref=recv.at[blocks, me],
+            send_sem=cross_send.at[j], recv_sem=cross_recv.at[j],
+            device_id={"tm": to, "chan": across}, device_id_type=mesh_id)
 
     def landed(b):
         def one(j, _):
@@ -180,21 +194,19 @@
 
     frames = wv.shape[1]
     half = frames // 2
-    zx = piece(0, mine, 0, frames, across)
-    own_r = piece(1, mine, 0, frames, right)
-    own_l = piece(2, mine, 0, frames, left)
-    far_r = piece(3, across, 0, frames, right)
-    far_l = piece(4, across, 0, frames, left)
     left_across = lax.rem(across + 6, 8)
     right_across = lax.rem(across + 2, 8)
-    own_rr = piece(5, left, 0, half, right)
-    own_ll = piece(6, right, half, half, left)
-    far_rr = piece(7, left_across, 0, half, right)
-    far_ll = piece(8, right_across, half, half, left)
-
-    def proof_block():
-        landed(0)
-        gather_rows(recv.at[0], rows)
+    own_r = piece(0, mine, 0, frames, right)
+    own_l = piece(1, mine, 0, frames, left)
+    far_r = piece(2, across, 0, frames, right)
+    far_l = piece(3, across, 0, frames, left)
+    own_rr = piece(4, left, 0, half, right)
+    own_ll = piece(5, right, half, half, left)
+    far_rr = piece(6, left_across, 0, half, right)
+    far_ll = piece(7, right_across, half, half, left)
+
+    def proof_piece(b, g):
+        gather_rows(recv.at[b], rows)
         power = []
         for w in range(8):
             r = rows[w]
@@ -203,23 +215,36 @@
             mat_re[pl.ds(w, 256, stride=16), :] = t[:, :128]
             mat_re[pl.ds(8 + w, 256, stride=16), :] = t[:, 128:]
 
-        def one(f, _):
-            wv[mine, f] = mat_re[pl.ds(pl.multiple_of(f * 16, 16), 16), :].astype(jnp.bfloat16)
-            return 0
-        lax.fori_loop(0, 256, one, 0)
+        def one(i, _):
+            for u in range(8):
+                f = i * 8 + u
+                wv[g, f] = mat_re[pl.ds(pl.multiple_of(f * 16, 16), 16), :].astype(jnp.bfloat16)
+            return 0
+        lax.fori_loop(0, 32, one, 0)
         rest = jnp.concatenate(power, axis=0)
         zero = jnp.zeros((8, 128), jnp.float32)
         for term in range(3):
             top = rest.astype(jnp.bfloat16).astype(jnp.float32)
             for h in range(2):
-                wv[mine, 256 + 3 * h + term] = jnp.concatenate(
+                wv[g, 256 + 3 * h + term] = jnp.concatenate(
                     [top[:, 128 * h:128 * h + 128], zero], axis=0).astype(jnp.bfloat16)
             rest = rest - top
         for i in range(262, frames):
-            wv[mine, i] = jnp.zeros((16, 128), jnp.bfloat16)
-        zx.start()
+            wv[g, i] = jnp.zeros((16, 128), jnp.bfloat16)
+
+    def proof_block():
+        landed(0)
+        proof_piece(0, mine)
         own_r.start()
         own_l.start()
+
+        def one(j, _):
+            cross_copy(j).wait_recv()
+            return 0
+        lax.fori_loop(0, peers, one, 0)
+        proof_piece(blocks, across)
+        far_r.start()
+        far_l.start()
 
     def aux_block(b):
         landed(b)
@@ -238,14 +263,32 @@
         mean8 = means[b]
 
         def step(s, _):
+            @pl.when(s == 7)
+            def _():
+                halo(b, aux.at[0]).wait()
             fft_step(x2d, b * 2304, mean8, scr, s, tabs)
             return 0
 
         lax.fori_loop(0, 8, step, 0)
 
+        @pl.when(b == 0)
+        def _():
+            total_means()
+
         @pl.when(b >= slots)
         def _():
             drain(b - slots)
+
+        @pl.when(b == slots)
+        def _():
+            def one(j, _):
+                cross_copy(j).wait_send()
+                return 0
+            lax.fori_loop(0, peers, one, 0)
+
+        diff = diffs[b]
+        shift = jnp.concatenate([jnp.broadcast_to(diff[c:c + 1], (8, 128)) for c in range(8)], axis=0)
+        scr[0:64, :] = scr[0:64, :] + shift * hann_bins
 
         def pack(d, _):
             for part in range(2):
@@ -264,7 +307,14 @@
         lax.fori_loop(1, peers, go, 0)
         recv[b, me] = send[slot, me]
 
-        @pl.when(b == 1)
+        @pl.when(b == 0)
+        def _():
+            def cross(j, _):
+                cross_copy(j).start()
+                return 0
+            lax.fori_loop(0, peers, cross, 0)
+
+        @pl.when(b == 2)
         def _():
             proof_block()
 
@@ -272,20 +322,14 @@
         def _():
             aux_block(b - 2)
 
-        @pl.when(b == 4)
-        def _():
-            zx.wait_recv()
-            far_r.start()
-            far_l.start()
-
-        @pl.when(b == 5)
+        @pl.when(b == 6)
         def _():
             own_r.wait_recv()
             own_l.wait_recv()
             own_rr.start()
             own_ll.start()
 
-        @pl.when(b == 7)
+        @pl.when(b == 8)
         def _():
             far_r.wait_recv()
             far_l.wait_recv()
@@ -329,19 +373,19 @@
 
         lax.fori_loop(b0, b0 + nb, emit, 0)
 
+    aux_block(7)
     own_rr.wait_recv()
     own_ll.wait_recv()
     far_rr.wait_recv()
     far_ll.wait_recv()
-    finish(0, 4)
-    aux_block(7)
+    finish(0, 7)
     aux_block(8)
-    finish(4, 4)
+    finish(7, 1)
     for h in range(2):
         for g in range(8):
             v = [wv[g, 256 + 3 * h + term].astype(jnp.float32)[:8] for term in range(3)]
             wpow[8 * g:8 * g + 8, 128 * h:128 * h + 128] = v[0] + v[1] + v[2]
-    for cp in (zx, own_r, own_l, far_r, far_l, own_rr, own_ll, far_rr, far_ll):
+    for cp in (own_r, own_l, far_r, far_l, own_rr, own_ll, far_rr, far_ll):
         cp.wait_send()
     for b in range(blocks - slots, blocks):
         drain(b)
@@ -384,8 +428,9 @@
             pltpu.VMEM((blocks, 288, 8, 128), f32),
             pltpu.VMEM((64 * PITCH, 128), f32),
             pltpu.VMEM((slots, peers, 2, 64, 256), bf16),
-            pltpu.VMEM((blocks, peers, 2, 64, 256), bf16),
+            pltpu.VMEM((blocks + 1, peers, 2, 64, 256), bf16),
             pltpu.VMEM((peers, 8, 128), f32),
+            pltpu.VMEM((blocks, 8, 128), f32),
             pltpu.VMEM((blocks, 8, 128), f32),
             pltpu.VMEM((8, 256, 256), f32),
             pltpu.VMEM((256 * PITCH, 128), f32),
@@ -395,7 +440,7 @@
             dma((blocks,)), dma((blocks,)), dma((blocks,)),
             dma((peers,)), dma((peers,)),
             dma((slots, peers)), dma((blocks, peers)),
-            dma((9,)), dma((9,)), dma((2,)),
+            dma((peers,)), dma((peers,)), dma((8,)), dma((8,)), dma((2,)),
         ],
         compiler_params=pltpu.CompilerParams(
             collective_id=0, has_side_effects=True, vmem_limit_bytes=63 * 2 ** 20),

time: 198 us -> 185 us (0.934); the launches traced: 195 us -> 185 us
  Pallas kernels: 188 us -> 177 us
    pallas_call x1, Pallas kernels: 188 us -> 177 us  [fused(): pl.pallas_call(functools.partial(fused_kernel, peers), out_shape=(jax.Sha...]
where the time goes in v3:
time: 185 us
  Pallas kernels  177 us (96%)
  other arithmetic  7.52 us (4%)
    pallas_call x1, Pallas kernels, fused(): pl.pallas_call(functools.partial(fused_kernel, peers), out_shape=(jax.Sha...  177 us
    div x1, other arithmetic, per_device(): return num / ((apow[:, None, :] + 1e-06) * (wpow[None, :, :] + 1e-06))  5.15 us

profile of v3, /device:TPU:1, one launch (start us, length us, event | category | flops | bytes accessed | tf_op | source)
XLA Modules:
  0.0 184.6 jit_solution(5988990524855419768)
XLA Ops:
  0.0 0.7 fusion.eye
  0.7 177.1 %shard_map.73 = (f32[64,64,256]{2,1,0:T(8,128)}, f32[8,8,256]{2,1,0:T(8,128)}, f32[64,256]{1,0:T(8,128)}) custom-call(f32[8,256,8,128]{3,2,1,0:T(8,128)} %bitcast.8, f32[1,256,8,128]{3,2,1,0:T(8,128)} %bitcast.9, bf16[256,256]{1,0:T(8,128)(2,1)} %fusion.eye, bf16[128,256]{1,0:T(8,128)(2,1)} %constant.22.f1, bf16[128,256]{1,0:T(8,128)(2,1)} %constant.27.w2, ...), custom_call_target="tpu_custom_call" | custom-call | tf_op jit(solution)/shard_map/pallas_call | solution.py:420
  177.7 0.8 add_bitcast_fusion
  178.6 0.8 broadcast_add_fusion
  179.4 5.2 %multiply_divide_fusion = f32[64,64,256]{2,1,0:T(8,128)} fusion(f32[64,64,256]{2,1,0:T(8,128)} %get-tuple-element.8, f32[64,256]{1,0:T(8,128)S(1)} %broadcast_add_fusion, f32[64,256]{1,0:T(8,128)S(1)} %add_bitcast_fusion), kind=kLoop, calls=%fused_computation | loop fusion | flops 2097152 | bytes 8519680 | tf_op jit(solution)/shard_map/div | solution.py:458

commit v4 on v3

--- a/solution.py
+++ b/solution.py
@@ -72,10 +72,10 @@
         scr[pl.ds(c * 8 + s, 64, stride=PITCH), :] = o[:, 128 * c:128 * c + 128]
 
 
-def fused_kernel(peers, aux, wit, eye, f1, w2, cos_t, sin_t, hann, num, apow, wpow,
-                 x, scr, send, recv, sums, means, diffs, rows, mat_re, mat_im, wv, tile,
+def fused_kernel(peers, aux, wit, f1, w2, cos_t, sin_t, hann, num, apow, wpow,
+                 x, scr, send, recv, sums, means, diffs, rows, mat_re, mat_im, wv, eye,
                  load_sem, halo_send, halo_recv, sum_send, sum_recv, send_sem, recv_sem,
-                 cross_send, cross_recv, ring_send, ring_recv, out_sem):
+                 half_send, half_recv, cross_send, cross_recv, ring_send, ring_recv):
     tabs = (f1, w2, cos_t, sin_t, hann)
     mesh_id = pl.DeviceIdType.MESH
     me = lax.axis_index("tm")
@@ -106,52 +106,57 @@
         cp = pltpu.make_async_copy(source(b), x.at[b, pl.ds(0, 256)], load_sem.at[b])
         cp.start()
         loads.append(cp)
-    pl.semaphore_wait(barrier, 2 * (peers - 1) + 3)
-
     def halo(b, src):
         return pltpu.make_async_remote_copy(
             src_ref=src.at[pl.ds(0, 32)], dst_ref=x.at[b, pl.ds(256, 32)],
             send_sem=halo_send.at[b], recv_sem=halo_recv.at[b],
             device_id={"tm": before}, device_id_type=mesh_id)
 
+    lane = lax.broadcasted_iota(jnp.int32, (8, 128), 1)
+
+    def block_sum(b):
+        def add(i, acc):
+            return acc + jnp.sum(x[b, pl.ds(i * 32, 32)].reshape(8, 4, 8, 128), axis=0)
+
+        part = jnp.sum(lax.fori_loop(0, 8, add, jnp.zeros((4, 8, 128), jnp.float32)), axis=0)
+        total = jnp.sum(part, axis=1, keepdims=True)
+        means[b] = jnp.broadcast_to(total / (256 * 128), (8, 128))
+        return total
+
+    def sum_copy(r, j):
+        return pltpu.make_async_remote_copy(
+            src_ref=sums.at[r, 0], dst_ref=sums.at[r, j],
+            send_sem=sum_send.at[r, j], recv_sem=sum_recv.at[r, j],
+            device_id={"tm": lax.rem(me + j, peers)}, device_id_type=mesh_id)
+
+    def sum_start(r):
+        def one(j, _):
+            sum_copy(r, j).start()
+            return 0
+        lax.fori_loop(1, peers, one, 0)
+
+    def total_means(r, which):
+        def one(j, acc):
+            sum_copy(r, j).wait()
+            return acc + sums[r, j]
+        total = lax.fori_loop(1, peers, one, sums[r, 0])
+        mean = total / (256 * 128 * peers)
+        for b in which:
+            diffs[b] = means[b] - jnp.broadcast_to(mean[:, b:b + 1], (8, 128))
+
+    loads[0].wait()
+    sums[0, 0] = jnp.where(lane == 0, block_sum(0), 0.0)
+    pl.semaphore_wait(barrier, 2 * (peers - 1) + 3)
     for b in range(blocks):
         halo(b, source(b)).start()
-
-    lane = lax.broadcasted_iota(jnp.int32, (8, 128), 1)
-    local = jnp.zeros((8, 128), jnp.float32)
-    for b in range(blocks):
-        loads[b].wait()
-
-        def add(i, acc):
-            return acc + jnp.sum(x[b, pl.ds(i * 32, 32)].reshape(8, 4, 8, 128), axis=0)
-
-        part = jnp.sum(lax.fori_loop(0, 8, add, jnp.zeros((4, 8, 128), jnp.float32)), axis=0)
-        local = jnp.where(lane == b, jnp.sum(part, axis=1, keepdims=True), local)
-    sums[0] = local
-    local_mean = local / (256 * 128)
-    for b in range(blocks):
-        means[b] = jnp.broadcast_to(local_mean[:, b:b + 1], (8, 128))
-
-    def sum_copy(j):
-        return pltpu.make_async_remote_copy(
-            src_ref=sums.at[0], dst_ref=sums.at[j], send_sem=sum_send.at[j], recv_sem=sum_recv.at[j],
-            device_id={"tm": lax.rem(me + j, peers)}, device_id_type=mesh_id)
-
-    def sum_start(j, _):
-        sum_copy(j).start()
-        return 0
-
-    def sum_wait(j, acc):
-        sum_copy(j).wait()
-        return acc + sums[j]
-
-    lax.fori_loop(1, peers, sum_start, 0)
-
-    def total_means():
-        total = lax.fori_loop(1, peers, sum_wait, sums[0])
-        mean = total / (256 * 128 * peers)
-        for b in range(blocks):
-            diffs[b] = means[b] - jnp.broadcast_to(mean[:, b:b + 1], (8, 128))
+    sum_start(0)
+    sums[1, 0] = jnp.zeros((8, 128), jnp.float32)
+    eye[...] = (lax.broadcasted_iota(jnp.int32, (128, 128), 0)
+                == lax.broadcasted_iota(jnp.int32, (128, 128), 1)).astype(jnp.float32).astype(jnp.bfloat16)
+
+    def other_sum(b):
+        pltpu.make_async_copy(aux.at[0], x.at[b, pl.ds(0, 256)], load_sem.at[b]).wait()
+        sums[1, 0] = jnp.where(lane == b, block_sum(b), sums[1, 0])
 
     x2d = x.reshape(blocks * 288 * 8, 128)
     row = lax.broadcasted_iota(jnp.int32, (64, 128), 0)
@@ -170,6 +175,22 @@
     def drain(b):
         def one(j, _):
             block_copy(b, j).wait_send()
+            return 0
+        lax.fori_loop(1, peers, one, 0)
+
+    def half_copy(hf, j):
+        to = lax.rem(me + 7 * j, peers)
+        return pltpu.make_async_remote_copy(
+            src_ref=send.at[(blocks - 1) % slots, to, hf], dst_ref=recv.at[blocks - 1, me, hf],
+            send_sem=half_send.at[hf, j], recv_sem=half_recv.at[hf, j],
+            device_id={"tm": to}, device_id_type=mesh_id)
+
+    def half_wait(hf, send_side):
+        def one(j, _):
+            if send_side:
+                half_copy(hf, j).wait_send()
+            else:
+                half_copy(hf, j).wait_recv()
             return 0
         lax.fori_loop(1, peers, one, 0)
 
@@ -206,14 +227,15 @@
     far_ll = piece(7, right_across, half, half, left)
 
     def proof_piece(b, g):
-        gather_rows(recv.at[b], rows)
         power = []
-        for w in range(8):
-            r = rows[w]
-            power.append(jnp.sum(r * r, axis=0, keepdims=True))
-            t = flip(eye[...], r)
-            mat_re[pl.ds(w, 256, stride=16), :] = t[:, :128]
-            mat_re[pl.ds(8 + w, 256, stride=16), :] = t[:, 128:]
+        for h in range(2):
+            gather_rows(recv.at[b], rows, h)
+            for w in range(8):
+                r = rows[w]
+                power.append(jnp.sum(r * r, axis=0, keepdims=True))
+                t = flip(eye[...], r)
+                mat_re[pl.ds(h * 2048 + w, 128, stride=16), :] = t[:, :128]
+                mat_re[pl.ds(h * 2048 + 8 + w, 128, stride=16), :] = t[:, 128:]
 
         def one(i, _):
             for u in range(8):
@@ -221,23 +243,23 @@
                 wv[g, f] = mat_re[pl.ds(pl.multiple_of(f * 16, 16), 16), :].astype(jnp.bfloat16)
             return 0
         lax.fori_loop(0, 32, one, 0)
-        rest = jnp.concatenate(power, axis=0)
         zero = jnp.zeros((8, 128), jnp.float32)
-        for term in range(3):
-            top = rest.astype(jnp.bfloat16).astype(jnp.float32)
-            for h in range(2):
-                wv[g, 256 + 3 * h + term] = jnp.concatenate(
-                    [top[:, 128 * h:128 * h + 128], zero], axis=0).astype(jnp.bfloat16)
-            rest = rest - top
+        for h in range(2):
+            rest = jnp.concatenate(power[8 * h:8 * h + 8], axis=0)
+            for term in range(3):
+                top = rest.astype(jnp.bfloat16).astype(jnp.float32)
+                wv[g, 256 + 3 * h + term] = jnp.concatenate([top, zero], axis=0).astype(jnp.bfloat16)
+                rest = rest - top
         for i in range(262, frames):
             wv[g, i] = jnp.zeros((16, 128), jnp.bfloat16)
 
-    def proof_block():
+    def proof_own():
         landed(0)
         proof_piece(0, mine)
         own_r.start()
         own_l.start()
 
+    def proof_across():
         def one(j, _):
             cross_copy(j).wait_recv()
             return 0
@@ -246,17 +268,21 @@
         far_r.start()
         far_l.start()
 
-    def aux_block(b):
-        landed(b)
-        gather_rows(recv.at[b], rows)
+    def aux_half(b, h):
+        gather_rows(recv.at[b], rows, h)
         e = eye[...]
         for c in range(8):
             r = rows[c]
-            apow[b - 1, c:c + 1, :] = jnp.sum(r * r, axis=0, keepdims=True)
+            apow[b - 1, c:c + 1, 128 * h:128 * h + 128] = jnp.sum(r * r, axis=0, keepdims=True)
             t = flip(e, r)
-            at = (b - 1) * 8 + c
-            mat_re[pl.ds(at, 256, stride=PITCH), :] = t[:, :128]
-            mat_im[pl.ds(at, 256, stride=PITCH), :] = t[:, 128:]
+            at = h * 128 * PITCH + (b - 1) * 8 + c
+            mat_re[pl.ds(at, 128, stride=PITCH), :] = t[:, :128]
+            mat_im[pl.ds(at, 128, stride=PITCH), :] = t[:, 128:]
+
+    def aux_block(b):
+        landed(b)
+        aux_half(b, 0)
+        aux_half(b, 1)
 
     def block(b, _):
         slot = lax.rem(b, slots)
@@ -267,13 +293,22 @@
             def _():
                 halo(b, aux.at[0]).wait()
             fft_step(x2d, b * 2304, mean8, scr, s, tabs)
+
+            @pl.when(b == 0)
+            def _():
+                other_sum(s + 1)
             return 0
 
         lax.fori_loop(0, 8, step, 0)
 
         @pl.when(b == 0)
         def _():
-            total_means()
+            sum_start(1)
+            total_means(0, range(1))
+
+        @pl.when(b == 1)
+        def _():
+            total_means(1, range(1, blocks))
 
         @pl.when(b >= slots)
         def _():
@@ -295,16 +330,26 @@
                 for hf in range(2):
                     at = pl.multiple_of((part * 32 + d * 2 + hf) * PITCH, 8)
                     v = scr[pl.ds(at, 64), :] * keep
-                    send[slot, d, part, :, hf * 128:hf * 128 + 128] = v.astype(jnp.bfloat16)
+                    send[slot, d, hf, part] = v.astype(jnp.bfloat16)
             return 0
 
         lax.fori_loop(0, peers, pack, 0)
 
-        def go(j, _):
-            block_copy(b, j).start()
-            return 0
-
-        lax.fori_loop(1, peers, go, 0)
+        @pl.when(b < blocks - 1)
+        def _():
+            def go(j, _):
+                block_copy(b, j).start()
+                return 0
+            lax.fori_loop(1, peers, go, 0)
+
+        @pl.when(b == blocks - 1)
+        def _():
+            for hf in range(2):
+                def go(j, _):
+                    half_copy(hf, j).start()
+                    return 0
+                lax.fori_loop(1, peers, go, 0)
+
         recv[b, me] = send[slot, me]
 
         @pl.when(b == 0)
@@ -314,22 +359,26 @@
                 return 0
             lax.fori_loop(0, peers, cross, 0)
 
+        @pl.when(b == 1)
+        def _():
+            proof_own()
+
         @pl.when(b == 2)
         def _():
-            proof_block()
+            proof_across()
 
         @pl.when(b >= 3)
         def _():
             aux_block(b - 2)
 
-        @pl.when(b == 6)
+        @pl.when(b == 5)
         def _():
             own_r.wait_recv()
             own_l.wait_recv()
             own_rr.start()
             own_ll.start()
 
-        @pl.when(b == 8)
+        @pl.when(b == 7)
         def _():
             far_r.wait_recv()
             far_l.wait_recv()
@@ -339,15 +388,13 @@
 
     lax.fori_loop(0, blocks, block, 0)
 
-    def store(b):
-        return pltpu.make_async_copy(tile.at[lax.rem(b, 2)], num.at[pl.ds(b * 8, 8)], out_sem.at[lax.rem(b, 2)])
-
-    def finish(b0, nb):
+    def finish(b0, nb, h):
         n = nb * 8
 
         def bins(i, _):
-            for u in range(8):
-                f = i * 8 + u
+            got = []
+            for u in range(32):
+                f = h * 128 + i * 32 + u
                 at = pl.ds(pl.multiple_of(f * PITCH + b0 * 8, 8), n)
                 lhs = jnp.concatenate([mat_re[at, :], mat_im[at, :]], axis=0).astype(jnp.bfloat16)
                 g = lax.dot_general(lhs, wv[:, f].reshape(128, 128), NT, preferred_element_type=jnp.float32)
@@ -357,46 +404,45 @@
                 mat_re[at, :] = re * re + im * im
             return 0
 
-        lax.fori_loop(0, 32, bins, 0)
+        lax.fori_loop(0, 4, bins, 0)
 
         def emit(b, _):
-            @pl.when(b >= 2)
-            def _():
-                store(b - 2).wait()
             for c in range(8):
-                for h in range(2):
-                    t = mat_re[pl.ds(h * 128 * PITCH + b * 8 + c, 128, stride=PITCH), :].T
-                    for g in range(8):
-                        tile[lax.rem(b, 2), c, 8 * g:8 * g + 8, 128 * h:128 * h + 128] = t[16 * g:16 * g + 8]
-            store(b).start()
+                t = mat_re[pl.ds(h * 128 * PITCH + b * 8 + c, 128, stride=PITCH), :].T
+                for g in range(8):
+                    num[b * 8 + c, 8 * g:8 * g + 8, 128 * h:128 * h + 128] = t[16 * g:16 * g + 8]
             return 0
 
         lax.fori_loop(b0, b0 + nb, emit, 0)
 
-    aux_block(7)
     own_rr.wait_recv()
     own_ll.wait_recv()
     far_rr.wait_recv()
     far_ll.wait_recv()
-    finish(0, 7)
-    aux_block(8)
-    finish(7, 1)
     for h in range(2):
         for g in range(8):
             v = [wv[g, 256 + 3 * h + term].astype(jnp.float32)[:8] for term in range(3)]
             wpow[8 * g:8 * g + 8, 128 * h:128 * h + 128] = v[0] + v[1] + v[2]
+    early = blocks - 3
+    for h in range(2):
+        finish(0, early, h)
+    aux_block(blocks - 2)
+    for h in range(2):
+        half_wait(h, False)
+        aux_half(blocks - 1, h)
+        finish(early, 2, h)
     for cp in (own_r, own_l, far_r, far_l, own_rr, own_ll, far_rr, far_ll):
         cp.wait_send()
-    for b in range(blocks - slots, blocks):
+    for b in range(blocks - slots, blocks - 1):
         drain(b)
-    store(6).wait()
-    store(7).wait()
-
-
-def gather_rows(stage, rows):
+    for h in range(2):
+        half_wait(h, True)
+
+
+def gather_rows(stage, rows, h):
     def one(t, _):
         for part in range(2):
-            v = stage[t, part].astype(jnp.float32)
+            v = stage[t, h, part].astype(jnp.float32)
             at = pl.multiple_of(part * 128 + t * 8, 8)
             for c in range(8):
                 rows[c, pl.ds(at, 8), :] = v[8 * c:8 * c + 8]
@@ -410,7 +456,6 @@
 
 def fused(aux, wit, peers):
     tabs = fft_tables()
-    eye = jnp.eye(256, dtype=jnp.bfloat16)
     vm = pl.BlockSpec(memory_space=pltpu.VMEM)
     hbm = pl.BlockSpec(memory_space=pl.ANY)
     blocks = aux.shape[0] + 1
@@ -422,29 +467,30 @@
         out_shape=(jax.ShapeDtypeStruct((64, 64, 256), f32),
                    jax.ShapeDtypeStruct((8, 8, 256), f32),
                    jax.ShapeDtypeStruct((64, 256), f32)),
-        in_specs=[hbm, hbm] + [vm] * 6,
-        out_specs=(hbm, vm, vm),
+        in_specs=[hbm, hbm] + [vm] * 5,
+        out_specs=(vm, vm, vm),
         scratch_shapes=[
             pltpu.VMEM((blocks, 288, 8, 128), f32),
             pltpu.VMEM((64 * PITCH, 128), f32),
-            pltpu.VMEM((slots, peers, 2, 64, 256), bf16),
-            pltpu.VMEM((blocks + 1, peers, 2, 64, 256), bf16),
-            pltpu.VMEM((peers, 8, 128), f32),
+            pltpu.VMEM((slots, peers, 2, 2, 64, 128), bf16),
+            pltpu.VMEM((blocks + 1, peers, 2, 2, 64, 128), bf16),
+            pltpu.VMEM((2, peers, 8, 128), f32),
             pltpu.VMEM((blocks, 8, 128), f32),
             pltpu.VMEM((blocks, 8, 128), f32),
-            pltpu.VMEM((8, 256, 256), f32),
+            pltpu.VMEM((8, 256, 128), f32),
             pltpu.VMEM((256 * PITCH, 128), f32),
             pltpu.VMEM((256 * PITCH, 128), f32),
             pltpu.VMEM((8, 264, 16, 128), bf16),
-            pltpu.VMEM((2, 8, 64, 256), f32),
+            pltpu.VMEM((128, 128), bf16),
             dma((blocks,)), dma((blocks,)), dma((blocks,)),
-            dma((peers,)), dma((peers,)),
+            dma((2, peers)), dma((2, peers)),
             dma((slots, peers)), dma((blocks, peers)),
-            dma((peers,)), dma((peers,)), dma((8,)), dma((8,)), dma((2,)),
+            dma((2, peers)), dma((2, peers)),
+            dma((peers,)), dma((peers,)), dma((8,)), dma((8,)),
         ],
         compiler_params=pltpu.CompilerParams(
             collective_id=0, has_side_effects=True, vmem_limit_bytes=63 * 2 ** 20),
-    )(aux, wit, eye, *tabs)
+    )(aux, wit, *tabs)
 
 
 def tiles(a):

time: 185 us -> 167 us (0.903)
  Pallas kernels: 177 us -> 160 us
    pallas_call x1, Pallas kernels: 177 us -> 160 us  [fused(): pl.pallas_call(functools.partial(fused_kernel, peers), out_shape=(jax.Sha...]
where the time goes in v4:
time: 167 us
  Pallas kernels  160 us (96%)
  other arithmetic  6.84 us (4%)
    pallas_call x1, Pallas kernels, fused(): pl.pallas_call(functools.partial(fused_kernel, peers), out_shape=(jax.Sha...  160 us
    div x1, other arithmetic, per_device(): return num / ((apow[:, None, :] + 1e-06) * (wpow[None, :, :] + 1e-06))  5.15 us

profile of v4, /device:TPU:1, one launch (start us, length us, event | category | flops | bytes accessed | tf_op | source)
XLA Modules:
  0.0 166.8 jit_solution(6938734551814808688)
XLA Ops:
  0.0 160.0 %shard_map.73 = (f32[64,64,256]{2,1,0:T(8,128)}, f32[8,8,256]{2,1,0:T(8,128)}, f32[64,256]{1,0:T(8,128)}) custom-call(f32[8,256,8,128]{3,2,1,0:T(8,128)} %bitcast.8, f32[1,256,8,128]{3,2,1,0:T(8,128)} %bitcast.9, bf16[128,256]{1,0:T(8,128)(2,1)} %constant.22.f1, bf16[128,256]{1,0:T(8,128)(2,1)} %constant.27.w2, f32[128,128]{1,0:T(8,128)} %constant.15.clone.cos_t, ...), custom_call_target="tpu_custom_call" | custom-call | tf_op jit(solution)/shard_map/pallas_call | solution.py:465
  160.0 0.8 add_bitcast_fusion
  160.8 0.8 broadcast_add_fusion
  161.7 5.2 %multiply_divide_fusion = f32[64,64,256]{2,1,0:T(8,128)} fusion(f32[64,64,256]{2,1,0:T(8,128)} %get-tuple-element.8, f32[64,256]{1,0:T(8,128)S(1)} %broadcast_add_fusion, f32[64,256]{1,0:T(8,128)S(1)} %add_bitcast_fusion), kind=kLoop, calls=%fused_computation | loop fusion | flops 2097152 | bytes 8519680 | tf_op jit(solution)/shard_map/div | solution.py:504

commit v5 on v4

--- a/solution.py
+++ b/solution.py
@@ -73,9 +73,9 @@
 
 
 def fused_kernel(peers, aux, wit, f1, w2, cos_t, sin_t, hann, num, apow, wpow,
-                 x, scr, send, recv, sums, means, diffs, rows, mat_re, mat_im, wv, eye,
+                 x, scr, send, recv, sums, means, diffs, rows, mat_re, mat_im, wv, eye, ybuf, numv,
                  load_sem, halo_send, halo_recv, sum_send, sum_recv, send_sem, recv_sem,
-                 half_send, half_recv, cross_send, cross_recv, ring_send, ring_recv):
+                 half_send, half_recv, y_send, y_recv, z_send, z_recv, ring_send, ring_recv, out_sem):
     tabs = (f1, w2, cos_t, sin_t, hann)
     mesh_id = pl.DeviceIdType.MESH
     me = lax.axis_index("tm")
@@ -84,6 +84,10 @@
     right = lax.rem(mine + 2, 8)
     left = lax.rem(mine + 6, 8)
     before = lax.rem(me + peers - 1, peers)
+    ring = peers // 2
+    spot = lax.rem(me, ring)
+    side = (me - spot) // ring
+    facing = (1 - side) * ring + spot
     blocks = x.shape[0]
     slots = send.shape[0]
 
@@ -95,10 +99,10 @@
     def greet(j, _):
         to = lax.rem(me + j, peers)
         pl.semaphore_signal(barrier, inc=1, device_id={"tm": to}, device_id_type=mesh_id)
-        pl.semaphore_signal(barrier, inc=1, device_id={"tm": to, "chan": across}, device_id_type=mesh_id)
         return 0
 
     lax.fori_loop(1, peers, greet, 0)
+    pl.semaphore_signal(barrier, inc=1, device_id={"tm": facing, "chan": across}, device_id_type=mesh_id)
     for c in (across, right, left):
         pl.semaphore_signal(barrier, inc=1, device_id={"chan": c}, device_id_type=mesh_id)
     loads = []
@@ -146,7 +150,7 @@
 
     loads[0].wait()
     sums[0, 0] = jnp.where(lane == 0, block_sum(0), 0.0)
-    pl.semaphore_wait(barrier, 2 * (peers - 1) + 3)
+    pl.semaphore_wait(barrier, peers - 1 + 4)
     for b in range(blocks):
         halo(b, source(b)).start()
     sum_start(0)
@@ -194,12 +198,36 @@
             return 0
         lax.fori_loop(1, peers, one, 0)
 
-    def cross_copy(j):
-        to = lax.rem(me + 7 * j, peers)
-        return pltpu.make_async_remote_copy(
-            src_ref=send.at[0, to], dst_ref=recv.at[blocks, me],
-            send_sem=cross_send.at[j], recv_sem=cross_recv.at[j],
-            device_id={"tm": to, "chan": across}, device_id_type=mesh_id)
+    def y_copy(k, j):
+        to = lax.rem(spot + 3 * j, ring)
+        return pltpu.make_async_remote_copy(
+            src_ref=send.at[0, k * ring + to], dst_ref=ybuf.at[k, spot],
+            send_sem=y_send.at[k, j], recv_sem=y_recv.at[k, j],
+            device_id={"tm": side * ring + to}, device_id_type=mesh_id)
+
+    def y_each(act):
+        def one(j, _):
+            for k in range(2):
+                act(y_copy(k, j))
+            return 0
+        lax.fori_loop(1, ring, one, 0)
+
+    def z_copy(i, k, b, dev):
+        return pltpu.make_async_remote_copy(
+            src_ref=ybuf.at[k], dst_ref=recv.at[b, pl.ds(side * ring, ring)],
+            send_sem=z_send.at[i], recv_sem=z_recv.at[i],
+            device_id=dev, device_id_type=mesh_id)
+
+    z_copies = [z_copy(0, 1 - side, 0, {"tm": facing}),
+                z_copy(1, 1 - side, blocks, {"tm": facing, "chan": across}),
+                z_copy(2, side, blocks, {"chan": across})]
+
+    def z_phase():
+        y_each(lambda cp: cp.wait_recv())
+        for cp in z_copies:
+            cp.start()
+        for i in range(ring):
+            recv[0, side * ring + i] = ybuf[side, i]
 
     def landed(b):
         def one(j, _):
@@ -254,16 +282,14 @@
             wv[g, i] = jnp.zeros((16, 128), jnp.bfloat16)
 
     def proof_own():
-        landed(0)
+        z_copies[0].wait_recv()
         proof_piece(0, mine)
         own_r.start()
         own_l.start()
 
     def proof_across():
-        def one(j, _):
-            cross_copy(j).wait_recv()
-            return 0
-        lax.fori_loop(0, peers, one, 0)
+        z_copies[1].wait_recv()
+        z_copies[2].wait_recv()
         proof_piece(blocks, across)
         far_r.start()
         far_l.start()
@@ -309,17 +335,15 @@
         @pl.when(b == 1)
         def _():
             total_means(1, range(1, blocks))
-
-        @pl.when(b >= slots)
+            z_phase()
+
+        @pl.when(b > slots)
         def _():
             drain(b - slots)
 
         @pl.when(b == slots)
         def _():
-            def one(j, _):
-                cross_copy(j).wait_send()
-                return 0
-            lax.fori_loop(0, peers, one, 0)
+            y_each(lambda cp: cp.wait_send())
 
         diff = diffs[b]
         shift = jnp.concatenate([jnp.broadcast_to(diff[c:c + 1], (8, 128)) for c in range(8)], axis=0)
@@ -335,7 +359,13 @@
 
         lax.fori_loop(0, peers, pack, 0)
 
-        @pl.when(b < blocks - 1)
+        @pl.when(b == 0)
+        def _():
+            y_each(lambda cp: cp.start())
+            for k in range(2):
+                ybuf[k, spot] = send[0, k * ring + spot]
+
+        @pl.when((b > 0) & (b < blocks - 1))
         def _():
             def go(j, _):
                 block_copy(b, j).start()
@@ -350,20 +380,15 @@
                     return 0
                 lax.fori_loop(1, peers, go, 0)
 
-        recv[b, me] = send[slot, me]
-
-        @pl.when(b == 0)
-        def _():
-            def cross(j, _):
-                cross_copy(j).start()
-                return 0
-            lax.fori_loop(0, peers, cross, 0)
-
-        @pl.when(b == 1)
+        @pl.when(b > 0)
+        def _():
+            recv[b, me] = send[slot, me]
+
+        @pl.when(b == 2)
         def _():
             proof_own()
 
-        @pl.when(b == 2)
+        @pl.when(b == 3)
         def _():
             proof_across()
 
@@ -378,7 +403,7 @@
             own_rr.start()
             own_ll.start()
 
-        @pl.when(b == 7)
+        @pl.when(b == 8)
         def _():
             far_r.wait_recv()
             far_l.wait_recv()
@@ -410,7 +435,7 @@
             for c in range(8):
                 t = mat_re[pl.ds(h * 128 * PITCH + b * 8 + c, 128, stride=PITCH), :].T
                 for g in range(8):
-                    num[b * 8 + c, 8 * g:8 * g + 8, 128 * h:128 * h + 128] = t[16 * g:16 * g + 8]
+                    numv[b * 8 + c, 8 * g:8 * g + 8, 128 * h:128 * h + 128] = t[16 * g:16 * g + 8]
             return 0
 
         lax.fori_loop(b0, b0 + nb, emit, 0)
@@ -426,17 +451,27 @@
     early = blocks - 3
     for h in range(2):
         finish(0, early, h)
+
+    def out_copy(i, b, n):
+        return pltpu.make_async_copy(numv.at[pl.ds(8 * b, 8 * n)], num.at[pl.ds(8 * b, 8 * n)], out_sem.at[i])
+
+    out_copy(0, 0, early).start()
     aux_block(blocks - 2)
     for h in range(2):
         half_wait(h, False)
         aux_half(blocks - 1, h)
         finish(early, 2, h)
+    out_copy(1, early, 2).start()
     for cp in (own_r, own_l, far_r, far_l, own_rr, own_ll, far_rr, far_ll):
         cp.wait_send()
     for b in range(blocks - slots, blocks - 1):
         drain(b)
     for h in range(2):
         half_wait(h, True)
+    for cp in z_copies:
+        cp.wait_send()
+    out_copy(0, 0, early).wait()
+    out_copy(1, early, 2).wait()
 
 
 def gather_rows(stage, rows, h):
@@ -468,7 +503,7 @@
                    jax.ShapeDtypeStruct((8, 8, 256), f32),
                    jax.ShapeDtypeStruct((64, 256), f32)),
         in_specs=[hbm, hbm] + [vm] * 5,
-        out_specs=(vm, vm, vm),
+        out_specs=(hbm, vm, vm),
         scratch_shapes=[
             pltpu.VMEM((blocks, 288, 8, 128), f32),
             pltpu.VMEM((64 * PITCH, 128), f32),
@@ -482,11 +517,14 @@
             pltpu.VMEM((256 * PITCH, 128), f32),
             pltpu.VMEM((8, 264, 16, 128), bf16),
             pltpu.VMEM((128, 128), bf16),
+            pltpu.VMEM((2, peers // 2, 2, 2, 64, 128), bf16),
+            pltpu.VMEM((64, 64, 256), f32),
             dma((blocks,)), dma((blocks,)), dma((blocks,)),
             dma((2, peers)), dma((2, peers)),
             dma((slots, peers)), dma((blocks, peers)),
             dma((2, peers)), dma((2, peers)),
-            dma((peers,)), dma((peers,)), dma((8,)), dma((8,)),
+            dma((2, peers // 2)), dma((2, peers // 2)), dma((3,)), dma((3,)),
+            dma((8,)), dma((8,)), dma((2,)),
         ],
         compiler_params=pltpu.CompilerParams(
             collective_id=0, has_side_effects=True, vmem_limit_bytes=63 * 2 ** 20),

time: 167 us -> 181 us (1.084); the launches traced: 167 us -> 178 us
  Pallas kernels: 160 us -> 171 us
    pallas_call x1, Pallas kernels: 160 us -> 171 us  [fused(): pl.pallas_call(functools.partial(fused_kernel, peers), out_shape=(jax.Sha...]
where the time goes in v5:
time: 181 us; the launch traced here: 178 us
  Pallas kernels  171 us (94%)
  other arithmetic  6.84 us (4%)
    pallas_call x1, Pallas kernels, fused(): pl.pallas_call(functools.partial(fused_kernel, peers), out_shape=(jax.Sha...  171 us
    div x1, other arithmetic, per_device(): return num / ((apow[:, None, :] + 1e-06) * (wpow[None, :, :] + 1e-06))  5.15 us

profile of v5, /device:TPU:1, one launch (start us, length us, event | category | flops | bytes accessed | tf_op | source)
XLA Modules:
  0.0 177.7 jit_solution(6877984894492323982)
XLA Ops:
  0.0 170.9 %shard_map.73 = (f32[64,64,256]{2,1,0:T(8,128)}, f32[8,8,256]{2,1,0:T(8,128)}, f32[64,256]{1,0:T(8,128)}) custom-call(f32[8,256,8,128]{3,2,1,0:T(8,128)} %bitcast.8, f32[1,256,8,128]{3,2,1,0:T(8,128)} %bitcast.9, bf16[128,256]{1,0:T(8,128)(2,1)} %constant.22.f1, bf16[128,256]{1,0:T(8,128)(2,1)} %constant.27.w2, f32[128,128]{1,0:T(8,128)} %constant.15.clone.cos_t, ...), custom_call_target="tpu_custom_call" | custom-call | tf_op jit(solution)/shard_map/pallas_call | solution.py:500
  170.9 0.8 add_bitcast_fusion
  171.7 0.8 broadcast_add_fusion
  172.6 5.2 %multiply_divide_fusion = f32[64,64,256]{2,1,0:T(8,128)} fusion(f32[64,64,256]{2,1,0:T(8,128)} %get-tuple-element.8, f32[64,256]{1,0:T(8,128)S(1)} %broadcast_add_fusion, f32[64,256]{1,0:T(8,128)S(1)} %add_bitcast_fusion), kind=kLoop, calls=%fused_computation | loop fusion | flops 2097152 | bytes 8519680 | tf_op jit(solution)/shard_map/div | solution.py:542

commit v6 on v4

--- a/solution.py
+++ b/solution.py
@@ -73,9 +73,9 @@
 
 
 def fused_kernel(peers, aux, wit, f1, w2, cos_t, sin_t, hann, num, apow, wpow,
-                 x, scr, send, recv, sums, means, diffs, rows, mat_re, mat_im, wv, eye,
+                 x, scr, send, recv, sums, means, diffs, rows, mat_re, mat_im, wv, eye, numv,
                  load_sem, halo_send, halo_recv, sum_send, sum_recv, send_sem, recv_sem,
-                 half_send, half_recv, cross_send, cross_recv, ring_send, ring_recv):
+                 half_send, half_recv, cross_send, cross_recv, ring_send, ring_recv, out_sem):
     tabs = (f1, w2, cos_t, sin_t, hann)
     mesh_id = pl.DeviceIdType.MESH
     me = lax.axis_index("tm")
@@ -84,7 +84,9 @@
     right = lax.rem(mine + 2, 8)
     left = lax.rem(mine + 6, 8)
     before = lax.rem(me + peers - 1, peers)
+    after = lax.rem(me + 1, peers)
     blocks = x.shape[0]
+    turn = (blocks + 1) // 2
     slots = send.shape[0]
 
     def source(b):
@@ -103,20 +105,22 @@
         pl.semaphore_signal(barrier, inc=1, device_id={"chan": c}, device_id_type=mesh_id)
     loads = []
     for b in range(blocks):
-        cp = pltpu.make_async_copy(source(b), x.at[b, pl.ds(0, 256)], load_sem.at[b])
+        cp = pltpu.make_async_copy(source(b), x.at[b, pl.ds(32 if b >= turn else 0, 256)], load_sem.at[b])
         cp.start()
         loads.append(cp)
-    def halo(b, src):
+    def halo(b, src, late):
         return pltpu.make_async_remote_copy(
-            src_ref=src.at[pl.ds(0, 32)], dst_ref=x.at[b, pl.ds(256, 32)],
+            src_ref=src.at[pl.ds(224 if late else 0, 32)], dst_ref=x.at[b, pl.ds(0 if late else 256, 32)],
             send_sem=halo_send.at[b], recv_sem=halo_recv.at[b],
-            device_id={"tm": before}, device_id_type=mesh_id)
+            device_id={"tm": after if late else before}, device_id_type=mesh_id)
 
     lane = lax.broadcasted_iota(jnp.int32, (8, 128), 1)
 
     def block_sum(b):
+        first = jnp.where(b >= turn, 32, 0)
+
         def add(i, acc):
-            return acc + jnp.sum(x[b, pl.ds(i * 32, 32)].reshape(8, 4, 8, 128), axis=0)
+            return acc + jnp.sum(x[b, pl.ds(first + i * 32, 32)].reshape(8, 4, 8, 128), axis=0)
 
         part = jnp.sum(lax.fori_loop(0, 8, add, jnp.zeros((4, 8, 128), jnp.float32)), axis=0)
         total = jnp.sum(part, axis=1, keepdims=True)
@@ -148,7 +152,7 @@
     sums[0, 0] = jnp.where(lane == 0, block_sum(0), 0.0)
     pl.semaphore_wait(barrier, 2 * (peers - 1) + 3)
     for b in range(blocks):
-        halo(b, source(b)).start()
+        halo(b, source(b), b >= turn).start()
     sum_start(0)
     sums[1, 0] = jnp.zeros((8, 128), jnp.float32)
     eye[...] = (lax.broadcasted_iota(jnp.int32, (128, 128), 0)
@@ -160,7 +164,8 @@
 
     x2d = x.reshape(blocks * 288 * 8, 128)
     row = lax.broadcasted_iota(jnp.int32, (64, 128), 0)
-    keep = jnp.where((lax.rem(row, 8) == 7) & (me == peers - 1), 0.0, 1.0)
+    keep_next = jnp.where((lax.rem(row, 8) == 7) & (me == peers - 1), 0.0, 1.0)
+    keep_last = jnp.where((lax.rem(row, 8) == 0) & (me == 0), 0.0, 1.0)
     col = lax.broadcasted_iota(jnp.int32, (64, 128), 1)
     hann_bins = jnp.where(col == 0, 4096.0, jnp.where(col == 1, -2048.0, 0.0))
 
@@ -270,14 +275,15 @@
 
     def aux_half(b, h):
         gather_rows(recv.at[b], rows, h)
+        back = jnp.where(b >= turn, 127, 0)
         e = eye[...]
         for c in range(8):
             r = rows[c]
             apow[b - 1, c:c + 1, 128 * h:128 * h + 128] = jnp.sum(r * r, axis=0, keepdims=True)
             t = flip(e, r)
             at = h * 128 * PITCH + (b - 1) * 8 + c
-            mat_re[pl.ds(at, 128, stride=PITCH), :] = t[:, :128]
-            mat_im[pl.ds(at, 128, stride=PITCH), :] = t[:, 128:]
+            mat_re[pl.ds(at, 128, stride=PITCH), :] = pltpu.roll(t[:, :128], back, 1)
+            mat_im[pl.ds(at, 128, stride=PITCH), :] = pltpu.roll(t[:, 128:], back, 1)
 
     def aux_block(b):
         landed(b)
@@ -289,9 +295,13 @@
         mean8 = means[b]
 
         def step(s, _):
-            @pl.when(s == 7)
+            @pl.when((s == 7) & (b < turn))
             def _():
-                halo(b, aux.at[0]).wait()
+                halo(b, aux.at[0], False).wait()
+
+            @pl.when((s == 0) & (b >= turn))
+            def _():
+                halo(b, aux.at[0], True).wait()
             fft_step(x2d, b * 2304, mean8, scr, s, tabs)
 
             @pl.when(b == 0)
@@ -324,6 +334,8 @@
         diff = diffs[b]
         shift = jnp.concatenate([jnp.broadcast_to(diff[c:c + 1], (8, 128)) for c in range(8)], axis=0)
         scr[0:64, :] = scr[0:64, :] + shift * hann_bins
+
+        keep = jnp.where(b >= turn, keep_last, keep_next)
 
         def pack(d, _):
             for part in range(2):
@@ -410,7 +422,7 @@
             for c in range(8):
                 t = mat_re[pl.ds(h * 128 * PITCH + b * 8 + c, 128, stride=PITCH), :].T
                 for g in range(8):
-                    num[b * 8 + c, 8 * g:8 * g + 8, 128 * h:128 * h + 128] = t[16 * g:16 * g + 8]
+                    numv[b * 8 + c, 8 * g:8 * g + 8, 128 * h:128 * h + 128] = t[16 * g:16 * g + 8]
             return 0
 
         lax.fori_loop(b0, b0 + nb, emit, 0)
@@ -426,17 +438,25 @@
     early = blocks - 3
     for h in range(2):
         finish(0, early, h)
+
+    def out_copy(i, b, n):
+        return pltpu.make_async_copy(numv.at[pl.ds(8 * b, 8 * n)], num.at[pl.ds(8 * b, 8 * n)], out_sem.at[i])
+
+    out_copy(0, 0, early).start()
     aux_block(blocks - 2)
     for h in range(2):
         half_wait(h, False)
         aux_half(blocks - 1, h)
         finish(early, 2, h)
+    out_copy(1, early, 2).start()
     for cp in (own_r, own_l, far_r, far_l, own_rr, own_ll, far_rr, far_ll):
         cp.wait_send()
     for b in range(blocks - slots, blocks - 1):
         drain(b)
     for h in range(2):
         half_wait(h, True)
+    out_copy(0, 0, early).wait()
+    out_copy(1, early, 2).wait()
 
 
 def gather_rows(stage, rows, h):
@@ -468,7 +488,7 @@
                    jax.ShapeDtypeStruct((8, 8, 256), f32),
                    jax.ShapeDtypeStruct((64, 256), f32)),
         in_specs=[hbm, hbm] + [vm] * 5,
-        out_specs=(vm, vm, vm),
+        out_specs=(hbm, vm, vm),
         scratch_shapes=[
             pltpu.VMEM((blocks, 288, 8, 128), f32),
             pltpu.VMEM((64 * PITCH, 128), f32),
@@ -482,17 +502,36 @@
             pltpu.VMEM((256 * PITCH, 128), f32),
             pltpu.VMEM((8, 264, 16, 128), bf16),
             pltpu.VMEM((128, 128), bf16),
+            pltpu.VMEM((64, 64, 256), f32),
             dma((blocks,)), dma((blocks,)), dma((blocks,)),
             dma((2, peers)), dma((2, peers)),
             dma((slots, peers)), dma((blocks, peers)),
             dma((2, peers)), dma((2, peers)),
-            dma((peers,)), dma((peers,)), dma((8,)), dma((8,)),
+            dma((peers,)), dma((peers,)), dma((8,)), dma((8,)), dma((2,)),
         ],
         compiler_params=pltpu.CompilerParams(
             collective_id=0, has_side_effects=True, vmem_limit_bytes=63 * 2 ** 20),
     )(aux, wit, *tabs)
 
 
+def divide_kernel(num, apow, wpow, out):
+    out[...] = num[...] / ((apow[...][:, None, :] + 1e-06) * (wpow[...][None, :, :] + 1e-06))
+
+
+def divide(num, apow, wpow):
+    rows = 32
+    return pl.pallas_call(
+        divide_kernel,
+        grid=(num.shape[0] // rows,),
+        out_shape=jax.ShapeDtypeStruct(num.shape, jnp.float32),
+        in_specs=[pl.BlockSpec((rows, 64, 256), lambda i: (i, 0, 0)),
+                  pl.BlockSpec((rows, 256), lambda i: (i, 0)),
+                  pl.BlockSpec((64, 256), lambda i: (0, 0))],
+        out_specs=pl.BlockSpec((rows, 64, 256), lambda i: (i, 0, 0)),
+        compiler_params=pltpu.CompilerParams(vmem_limit_bytes=60 * 2 ** 20),
+    )(num, apow, wpow)
+
+
 def tiles(a):
     return a.reshape(a.shape[0] // 8, 8, 256, 128).transpose(0, 2, 1, 3)
 
@@ -501,7 +540,7 @@
     peers = lax.axis_size("tm")
     num, apow, wpow = fused(tiles(auxiliary), tiles(proofs), peers)
     apow = apow.reshape(64, 256)
-    return num / ((apow[:, None, :] + 1e-06) * (wpow[None, :, :] + 1e-06))
+    return divide(num, apow, wpow)
 
 
 def solution(mesh):

time: 167 us -> 159 us (0.952)
  other arithmetic: 6.84 us -> 0 us
    pallas_call x1, Pallas kernels: 160 us -> 155 us  [fused(): pl.pallas_call(functools.partial(fused_kernel, peers), out_shape=(jax.Sha...]
    div x1 -> x0, other arithmetic: 5.15 us -> none  [per_device(): return num / ((apow[:, None, :] + 1e-06) * (wpow[None, :, :] + 1e-06))]
    pallas_call x0 -> x1, Pallas kernels: none -> 3.9 us  [divide(): pl.pallas_call(divide_kernel, grid=(num.shape[0] // rows,), out_shape=jax...]
    add x2 -> x0, other arithmetic: 1.69 us -> none  [per_device(): return num / ((apow[:, None, :] + 1e-06) * (wpow[None, :, :] + 1e-06))]
where the time goes in v6:
time: 159 us
  Pallas kernels  159 us (100%)
    pallas_call x1, Pallas kernels, fused(): pl.pallas_call(functools.partial(fused_kernel, peers), out_shape=(jax.Sha...  155 us
    pallas_call x1, Pallas kernels, divide(): pl.pallas_call(divide_kernel, grid=(num.shape[0] // rows,), out_shape=jax...  3.9 us

profile of v6, /device:TPU:1, one launch (start us, length us, event | category | flops | bytes accessed | tf_op | source)
XLA Modules:
  0.0 158.6 jit_solution(9083175599204818022)
XLA Ops:
  0.0 154.7 %shard_map.73 = (f32[64,64,256]{2,1,0:T(8,128)}, f32[8,8,256]{2,1,0:T(8,128)}, f32[64,256]{1,0:T(8,128)}) custom-call(f32[8,256,8,128]{3,2,1,0:T(8,128)} %bitcast.7, f32[1,256,8,128]{3,2,1,0:T(8,128)} %bitcast.8, bf16[128,256]{1,0:T(8,128)(2,1)} %constant.19.f1, bf16[128,256]{1,0:T(8,128)(2,1)} %constant.24.w2, f32[128,128]{1,0:T(8,128)} %constant.12.clone.cos_t, ...), custom_call_target="tpu_custom_call" | custom-call | tf_op jit(solution)/shard_map/pallas_call | solution.py:485
  154.7 3.9 %shard_map.74 = f32[64,64,256]{2,1,0:T(8,128)} custom-call(f32[64,64,256]{2,1,0:T(8,128)} %get-tuple-element.8.num, f32[64,256]{1,0:T(8,128)} %bitcast.9, f32[64,256]{1,0:T(8,128)} %get-tuple-element.10.wpow), custom_call_target="tpu_custom_call" | custom-call | tf_op jit(solution)/shard_map/pallas_call | solution.py:523

commit v7 on v6

--- a/solution.py
+++ b/solution.py
@@ -383,14 +383,14 @@
         def _():
             aux_block(b - 2)
 
-        @pl.when(b == 5)
+        @pl.when(b == 4)
         def _():
             own_r.wait_recv()
             own_l.wait_recv()
             own_rr.start()
             own_ll.start()
 
-        @pl.when(b == 7)
+        @pl.when(b == 6)
         def _():
             far_r.wait_recv()
             far_l.wait_recv()
@@ -402,11 +402,11 @@
 
     def finish(b0, nb, h):
         n = nb * 8
+        wide = 64 if nb <= 2 else 32
 
         def bins(i, _):
-            got = []
-            for u in range(32):
-                f = h * 128 + i * 32 + u
+            for u in range(wide):
+                f = h * 128 + i * wide + u
                 at = pl.ds(pl.multiple_of(f * PITCH + b0 * 8, 8), n)
                 lhs = jnp.concatenate([mat_re[at, :], mat_im[at, :]], axis=0).astype(jnp.bfloat16)
                 g = lax.dot_general(lhs, wv[:, f].reshape(128, 128), NT, preferred_element_type=jnp.float32)
@@ -416,7 +416,7 @@
                 mat_re[at, :] = re * re + im * im
             return 0
 
-        lax.fori_loop(0, 4, bins, 0)
+        lax.fori_loop(0, 128 // wide, bins, 0)
 
         def emit(b, _):
             for c in range(8):

time: 159 us -> 158 us (level)
  no operation moved by 1% of the time
where the time goes in v7:
time: 158 us
  Pallas kernels  158 us (100%)
    pallas_call x1, Pallas kernels, fused(): pl.pallas_call(functools.partial(fused_kernel, peers), out_shape=(jax.Sha...  154 us
    pallas_call x1, Pallas kernels, divide(): pl.pallas_call(divide_kernel, grid=(num.shape[0] // rows,), out_shape=jax...  3.9 us

profile of v7, /device:TPU:1, one launch (start us, length us, event | category | flops | bytes accessed | tf_op | source)
XLA Modules:
  0.0 157.9 jit_solution(99744508607758213)
XLA Ops:
  0.0 154.0 %shard_map.73 = (f32[64,64,256]{2,1,0:T(8,128)}, f32[8,8,256]{2,1,0:T(8,128)}, f32[64,256]{1,0:T(8,128)}) custom-call(f32[8,256,8,128]{3,2,1,0:T(8,128)} %bitcast.7, f32[1,256,8,128]{3,2,1,0:T(8,128)} %bitcast.8, bf16[128,256]{1,0:T(8,128)(2,1)} %constant.19.f1, bf16[128,256]{1,0:T(8,128)(2,1)} %constant.24.w2, f32[128,128]{1,0:T(8,128)} %constant.12.clone.cos_t, ...), custom_call_target="tpu_custom_call" | custom-call | tf_op jit(solution)/shard_map/pallas_call | solution.py:485
  154.0 3.9 %shard_map.74 = f32[64,64,256]{2,1,0:T(8,128)} custom-call(f32[64,64,256]{2,1,0:T(8,128)} %get-tuple-element.8.num, f32[64,256]{1,0:T(8,128)} %bitcast.9, f32[64,256]{1,0:T(8,128)} %get-tuple-element.10.wpow), custom_call_target="tpu_custom_call" | custom-call | tf_op jit(solution)/shard_map/pallas_call | solution.py:523
